TPU v7x, 512 devices: a 4x2x32 block of a 4x8x32 slice. The times are simulated.
512 devices in a mesh: scen: 2 (over y), row: 32 (over z), col: 4 (over x), layer: 2 (over core).
Axes of the slice: x: 4, y: 2, z: 32, core: 2. Of those that a mesh axis runs over, the one named last changes fastest.
The devices are a block of a 4x8x32 slice.
Arguments:
- current: float32 [2, 8192, 4096], P('layer', ('scen', 'row'), 'col'), parts along dimension 1, may hold values from 0.5 to 10
- node_class: int32 [2, 8192, 4096], P('layer', ('scen', 'row'), 'col'), parts along dimension 1, may hold values from 0 to 7
- class_conductance: float32 [2, 8], P('layer'), may hold values from 0.5 to 4
- pad_mask: int32 [2, 8192, 4096], P('layer', ('scen', 'row'), 'col'), parts along dimension 1, may hold values 0 or 1
- via_mask: int32 [8192, 4096], P(('scen', 'row'), 'col'), parts along dimension 0, may hold values 0 or 1
Outputs:
- drop: float32 [2, 8192, 4096], P('layer', ('scen', 'row'), 'col'), parts along dimension 1
- residual: float32 [2, 8192, 4096], P('layer', ('scen', 'row'), 'col'), parts along dimension 1
- worst: float32 [2, 8192, 4096], P('layer', ('scen', 'row'), 'col'), parts along dimension 1
There are 2 independent parts, one for each index of `scen`. A program takes and returns all parts, laid end to end along the dimension named above; an argument that names none is the same for every part. Nothing has to cross between parts.
All inputs are finite; a program needn't handle non-finite values. No bound on the sum of `pad_mask` or of `via_mask` on one device may be relied on, other than what follows from the above.
Results may differ from a plain program's by a relative error of at most 0.0003.
Values sent between devices are 32-bit elements; how exact they have to be, the bound alone decides.
A program may use at most 64 MiB of HBM per device.

v0:
```python
import functools

import jax
import jax.numpy as jnp
from jax import lax
from jax.sharding import PartitionSpec as P

ITERS = 2


via_conductance = 2.0
pad_conductance = 4.0
leakage = 0.05


def with_halo(value, sides, width):
    edges = {}
    for axis, dim in sides:
        size, length = (lax.axis_size(axis), value.shape[dim])
        up = [(i, (i + 1) % size) for i in range(size - 1)]
        last = lax.slice_in_dim(value, length - width, length, axis=dim)
        initial = lax.slice_in_dim(value, 0, width, axis=dim)
        edges[dim] = (
            lax.ppermute(last, axis, up),
            lax.ppermute(initial, axis, [(b, a) for a, b in up]),
        )
    done = []
    for _, dim in sides:
        low, high = edges[dim]
        around = [(width, width) if d in done else (0, 0) for d in range(value.ndim)]
        value = jnp.concatenate([jnp.pad(low, around), value, jnp.pad(high, around)], axis=dim)
        done.append(dim)
    return value


def from_partner(value, axis, stride):
    return lax.ppermute(value, axis, [(i, i ^ 1 << stride) for i in range(lax.axis_size(axis))])


def over_axes(value, axes):
    return functools.reduce(lax.psum, axes, value)


def lookup(node_class, class_conductance):
    cond = jnp.zeros(node_class.shape, jnp.float32)
    for klass in range(class_conductance.shape[1]):
        cond = cond + jnp.where(
            node_class == klass, class_conductance[:, klass][:, None, None], jnp.float32(0.0)
        )
    return cond


def edge_terms(cond):
    padded = with_halo(cond, (("row", 1), ("col", 2)), 1)
    beside_all = (
        padded[:, :-2, 1:-1],
        padded[:, 2:, 1:-1],
        padded[:, 1:-1, :-2],
        padded[:, 1:-1, 2:],
    )
    return tuple(
        (jnp.where(other > 0.0, 0.5 * (cond + other), jnp.float32(0.0)) for other in beside_all)
    )


def apply_grid(values, edges, diagonal, coupling):
    padded = with_halo(values, (("row", 1), ("col", 2)), 1)
    partner = from_partner(values, "layer", 0)
    beside = edges[0] * padded[:, :-2, 1:-1] + edges[1] * padded[:, 2:, 1:-1]
    beside = beside + edges[2] * padded[:, 1:-1, :-2] + edges[3] * padded[:, 1:-1, 2:]
    return diagonal * values - beside - coupling * partner


def local(current, node_class, class_conductance, pad_mask, via_mask):
    cond = lookup(node_class, class_conductance)
    edges = edge_terms(cond)
    coupling = via_conductance * via_mask.astype(jnp.float32)
    diagonal = (
        edges[0]
        + edges[1]
        + edges[2]
        + edges[3]
        + coupling
        + pad_conductance * pad_mask.astype(jnp.float32)
        + leakage
    )
    drop_field = jnp.zeros_like(current)
    resid = current
    worst_field = drop_field

    def inner_pair(resid_now):
        precond_now = resid_now / diagonal
        image_now = apply_grid(precond_now, edges, diagonal, coupling)
        energy_part, curve_part = (
            over_axes(jnp.sum(resid_now * precond_now), ("row", "col", "layer")),
            over_axes(jnp.sum(precond_now * image_now), ("row", "col", "layer")),
        )
        return (precond_now, image_now, energy_part, curve_part)

    precond, image, energy_now, curve_now = inner_pair(resid)
    step_size = energy_now / curve_now
    direction, along = (precond, image)
    for iteration in range(ITERS):
        drop_field = drop_field + step_size * direction
        resid = resid - step_size * along
        worst_field = drop_field if iteration == 0 else jnp.maximum(worst_field, drop_field)
        if iteration + 1 < ITERS:
            precond, image, energy_next, curve_now = inner_pair(resid)
            ratio = energy_next / energy_now
            step_size = energy_next / (curve_now - ratio * energy_next / step_size)
            direction = precond + ratio * direction
            along = image + ratio * along
            energy_now = energy_next
    return (drop_field, resid, worst_field)


def solution(mesh):
    in_specs = (
        P("layer", ("scen", "row"), "col"),
        P("layer", ("scen", "row"), "col"),
        P("layer", None),
        P("layer", ("scen", "row"), "col"),
        P(("scen", "row"), "col"),
    )
    out_specs = (
        P("layer", ("scen", "row"), "col"),
        P("layer", ("scen", "row"), "col"),
        P("layer", ("scen", "row"), "col"),
    )
    return jax.shard_map(local, mesh=mesh, in_specs=in_specs, out_specs=out_specs, check_vma=False)
```

profile of v0, /device:TPU:40, one launch (start us, length us, event | category | flops | bytes accessed | tf_op | source)
XLA Modules:
  0.0 247.4 jit_solution(104000323186430484)
XLA Ops:
  0.6 1.6 fusion.45
  2.3 0.0 copy-start
  2.3 0.0 copy-start.1
  2.3 6.6 %select_add_fusion = f32[1,128,1024]{2,1,0:T(8,128)S(1)} fusion(s32[1,128,1024]{2,1,0:T(8,128)} %param.6, f32[]{:T(128)} %bitcast.7, f32[]{:T(128)} %bitcast.6, f32[]{:T(128)} %bitcast.5, f32[]{:T(128)} %bitcast.4, f32[]{:T(128)} %bitcast.3, f32[]{:T(128)} %bitcast.2, f32[]{:T(128)} %bitcast.1, f32[]{:T(128)} %bitcast), kind=kLoop, calls=%fused_computation.73 | loop fusion | flops 3014656 | bytes 1048608 | tf_op jit(solution)/shard_map/add | solution.py:47
  8.8 4.7 %collective-permute-start = (f32[1,1,1024]{2,1,0:T(1,128)S(1)}, f32[1,1,1024]{2,1,0:T(1,128)S(1)}, u32[]{:S(2)}, u32[]{:S(2)}) collective-permute-start(f32[1,1,1024]{2,1,0:T(1,128)S(1)} %get-tuple-element.35), channel_id=1, source_target_pairs={{0,8},{8,16},{16,24},{24,32},{32,40},{40,48},{48,56},{56,64},{64,7... | collective-permute-start | bytes 12296 | tf_op jit(solution)/shard_map/ppermute | solution.py:24
  13.6 1.3 collective-permute-start.1
  14.9 0.1 fusion.43
  15.0 3.6 %collective-permute-start.2 = (f32[1,128,1]{2,1,0:T(8,128)S(1)}, f32[1,128,1]{2,1,0:T(8,128)S(1)}, u32[]{:S(2)}, u32[]{:S(2)}) collective-permute-start(f32[1,128,1]{2,1,0:T(8,128)S(1)} %get-tuple-element.33), channel_id=1, source_target_pairs={{0,2},{2,4},{4,6},{1,3},{3,5},{5,7},{8,10},{10,12},{12,14},{9,11},... | collective-permute-start | bytes 1544 | tf_op jit(solution)/shard_map/ppermute | solution.py:24
  18.5 1.3 collective-permute-start.3
  19.8 0.6 collective-permute-done.2
  20.4 4.3 %collective-permute-done.3 = f32[1,128,1]{2,1,0:T(8,128)S(1)} collective-permute-done((f32[1,128,1]{2,1,0:T(8,128)S(1)}, f32[1,128,1]{2,1,0:T(8,128)S(1)}, u32[]{:S(2)}, u32[]{:S(2)}) %collective-permute-start.3) | collective-permute-done | bytes 544 | tf_op jit(solution)/shard_map/ppermute | solution.py:25
  24.7 0.0 collective-permute-done
  24.7 0.0 collective-permute-done.1
  24.7 0.0 copy-done
  24.7 0.0 copy-done.1
  24.7 1.7 fusion.37
  26.4 2.0 collective-permute-start.8
  28.4 5.4 %collective-permute-start.4 = (f32[1,1,1024]{2,1,0:T(1,128)S(1)}, f32[1,1,1024]{2,1,0:T(1,128)S(1)}, u32[]{:S(2)}, u32[]{:S(2)}) collective-permute-start(f32[1,1,1024]{2,1,0:T(1,128)S(1)} %get-tuple-element.31), channel_id=1, source_target_pairs={{0,8},{8,16},{16,24},{24,32},{32,40},{40,48},{48,56},{56,64},{64,7... | collective-permute-start | bytes 12296 | tf_op jit(solution)/shard_map/ppermute | solution.py:24
  33.7 1.3 collective-permute-start.5
  35.1 0.1 fusion.41
  35.1 3.6 %collective-permute-start.6 = (f32[1,128,1]{2,1,0:T(8,128)S(1)}, f32[1,128,1]{2,1,0:T(8,128)S(1)}, u32[]{:S(2)}, u32[]{:S(2)}) collective-permute-start(f32[1,128,1]{2,1,0:T(8,128)S(1)} %get-tuple-element.29), channel_id=1, source_target_pairs={{0,2},{2,4},{4,6},{1,3},{3,5},{5,7},{8,10},{10,12},{12,14},{9,11},... | collective-permute-start | bytes 1544 | tf_op jit(solution)/shard_map/ppermute | solution.py:24
  38.7 1.3 collective-permute-start.7
  40.0 0.6 collective-permute-done.6
  40.6 4.3 %collective-permute-done.7 = f32[1,128,1]{2,1,0:T(8,128)S(1)} collective-permute-done((f32[1,128,1]{2,1,0:T(8,128)S(1)}, f32[1,128,1]{2,1,0:T(8,128)S(1)}, u32[]{:S(2)}, u32[]{:S(2)}) %collective-permute-start.7) | collective-permute-done | bytes 544 | tf_op jit(solution)/shard_map/ppermute | solution.py:25
  44.9 0.0 collective-permute-done.4
  44.9 0.0 collective-permute-done.5
  44.9 0.0 collective-permute-done.8
  44.9 1.5 multiply_reduce_fusion.2
  46.4 95.9 %all-reduce.7 = (f32[]{:T(128)}, f32[]{:T(128)}) all-reduce(f32[]{:T(128)} %get-tuple-element.6, f32[]{:T(128)} %get-tuple-element.5), channel_id=1, replica_groups=mesh['scen'=2,'row'=32,'col'=4,'layer'=2] {'row'}, use_global_device_ids=true, to_apply=%region_1.2 | all-reduce | flops 2 | bytes 16 | tf_op jit(solution)/shard_map/psum | solution.py:41
  142.3 9.7 %all-reduce.9 = (f32[]{:T(128)}, f32[]{:T(128)}) all-reduce(f32[]{:T(128)} %get-tuple-element.9, f32[]{:T(128)} %get-tuple-element.10), channel_id=1, replica_groups=mesh['scen'=2,'row'=32,'col'=4,'layer'=2] {'col'}, use_global_device_ids=true, to_apply=%region_2.3 | all-reduce | flops 2 | bytes 16 | tf_op jit(solution)/shard_map/psum | solution.py:41
  152.0 3.1 %all-reduce.11 = (f32[]{:T(128)}, f32[]{:T(128)}) all-reduce(f32[]{:T(128)} %get-tuple-element.13, f32[]{:T(128)} %get-tuple-element.14), channel_id=1, replica_groups=mesh['scen'=2,'row'=32,'col'=4,'layer'=2] {'layer'}, use_global_device_ids=true, to_apply=%region_3.4 | all-reduce | flops 2 | bytes 16 | tf_op jit(solution)/shard_map/psum | solution.py:41
  156.4 0.0 copy-start.2
  156.5 0.1 fusion.34
  156.6 2.1 collective-permute-start.13
  158.7 1.3 collective-permute-start.9
  160.0 1.3 collective-permute-start.10
  161.4 0.1 fusion.39
  161.4 2.6 %collective-permute-start.11 = (f32[1,128,1]{2,1,0:T(8,128)S(1)}, f32[1,128,1]{2,1,0:T(8,128)S(1)}, u32[]{:S(2)}, u32[]{:S(2)}) collective-permute-start(f32[1,128,1]{2,1,0:T(8,128)S(1)} %get-tuple-element.25), channel_id=1, source_target_pairs={{0,2},{2,4},{4,6},{1,3},{3,5},{5,7},{8,10},{10,12},{12,14},{9,11},... | collective-permute-start | bytes 1544 | tf_op jit(solution)/shard_map/ppermute | solution.py:24
  164.1 1.3 collective-permute-start.12
  165.4 0.6 collective-permute-done.11
  165.9 4.3 %collective-permute-done.12 = f32[1,128,1]{2,1,0:T(8,128)S(1)} collective-permute-done((f32[1,128,1]{2,1,0:T(8,128)S(1)}, f32[1,128,1]{2,1,0:T(8,128)S(1)}, u32[]{:S(2)}, u32[]{:S(2)}) %collective-permute-start.12) | collective-permute-done | bytes 544 | tf_op jit(solution)/shard_map/ppermute | solution.py:25
  170.3 0.0 collective-permute-done.9
  170.3 0.0 collective-permute-done.10
  170.3 0.0 collective-permute-done.13
  170.3 0.0 copy-done.2
  170.3 2.4 multiply_reduce_fusion
  172.6 56.3 %all-reduce.6 = (f32[]{:T(128)}, f32[]{:T(128)}) all-reduce(f32[]{:T(128)} %get-tuple-element.4, f32[]{:T(128)} %get-tuple-element.3), channel_id=1, replica_groups=mesh['scen'=2,'row'=32,'col'=4,'layer'=2] {'row'}, use_global_device_ids=true, to_apply=%region_9.10 | all-reduce | flops 2 | bytes 16 | tf_op jit(solution)/shard_map/psum | solution.py:41
  228.9 8.6 %all-reduce.8 = (f32[]{:T(128)}, f32[]{:T(128)}) all-reduce(f32[]{:T(128)} %get-tuple-element.7, f32[]{:T(128)} %get-tuple-element.8), channel_id=1, replica_groups=mesh['scen'=2,'row'=32,'col'=4,'layer'=2] {'col'}, use_global_device_ids=true, to_apply=%region_10.11 | all-reduce | flops 2 | bytes 16 | tf_op jit(solution)/shard_map/psum | solution.py:41
  237.5 3.1 %all-reduce.10 = (f32[]{:T(128)}, f32[]{:T(128)}) all-reduce(f32[]{:T(128)} %get-tuple-element.11, f32[]{:T(128)} %get-tuple-element.12), channel_id=1, replica_groups=mesh['scen'=2,'row'=32,'col'=4,'layer'=2] {'layer'}, use_global_device_ids=true, to_apply=%region_11.12 | all-reduce | flops 2 | bytes 16 | tf_op jit(solution)/shard_map/psum | solution.py:41
  245.1 2.3 multiply_maximum_fusion
  (3 shorter events, 0.0 us)
Async XLA Ops:
  2.3 22.5 %copy-start = (f32[1,128,1024]{2,1,0:T(8,128)S(1)}, f32[1,128,1024]{2,1,0:T(8,128)}, u32[]{:S(2)}) copy-start(f32[1,128,1024]{2,1,0:T(8,128)} %param.5) | copy-start | bytes 1572868
  2.3 22.5 %copy-start.1 = (s32[128,1024]{1,0:T(8,128)S(1)}, s32[128,1024]{1,0:T(8,128)}, u32[]{:S(2)}) copy-start(s32[128,1024]{1,0:T(8,128)} %param.9) | copy-start | bytes 1572868
  8.8 15.9 %collective-permute-start = (f32[1,1,1024]{2,1,0:T(1,128)S(1)}, f32[1,1,1024]{2,1,0:T(1,128)S(1)}, u32[]{:S(2)}, u32[]{:S(2)}) collective-permute-start(f32[1,1,1024]{2,1,0:T(1,128)S(1)} %get-tuple-element.35), channel_id=1, source_target_pairs={{0,8},{8,16},{16,24},{24,32},{32,40},{40,48},{48,56},{56,64},{64,7... | collective-permute-start | bytes 12296 | tf_op jit(solution)/shard_map/ppermute | solution.py:24
  13.6 11.2 %collective-permute-start.1 = (f32[1,1,1024]{2,1,0:T(1,128)S(1)}, f32[1,1,1024]{2,1,0:T(1,128)S(1)}, u32[]{:S(2)}, u32[]{:S(2)}) collective-permute-start(f32[1,1,1024]{2,1,0:T(1,128)S(1)} %get-tuple-element.36), channel_id=1, source_target_pairs={{8,0},{16,8},{24,16},{32,24},{40,32},{48,40},{56,48},{64,56},{72,6... | collective-permute-start | bytes 12296 | tf_op jit(solution)/shard_map/ppermute | solution.py:25
  15.0 5.5 %collective-permute-start.2 = (f32[1,128,1]{2,1,0:T(8,128)S(1)}, f32[1,128,1]{2,1,0:T(8,128)S(1)}, u32[]{:S(2)}, u32[]{:S(2)}) collective-permute-start(f32[1,128,1]{2,1,0:T(8,128)S(1)} %get-tuple-element.33), channel_id=1, source_target_pairs={{0,2},{2,4},{4,6},{1,3},{3,5},{5,7},{8,10},{10,12},{12,14},{9,11},... | collective-permute-start | bytes 1544 | tf_op jit(solution)/shard_map/ppermute | solution.py:24
  18.5 6.2 %collective-permute-start.3 = (f32[1,128,1]{2,1,0:T(8,128)S(1)}, f32[1,128,1]{2,1,0:T(8,128)S(1)}, u32[]{:S(2)}, u32[]{:S(2)}) collective-permute-start(f32[1,128,1]{2,1,0:T(8,128)S(1)} %get-tuple-element.34), channel_id=1, source_target_pairs={{2,0},{4,2},{6,4},{3,1},{5,3},{7,5},{10,8},{12,10},{14,12},{11,9},... | collective-permute-start | bytes 1544 | tf_op jit(solution)/shard_map/ppermute | solution.py:25
  26.4 18.5 %collective-permute-start.8 = (f32[1,128,1024]{2,1,0:T(8,128)S(1)}, f32[1,128,1024]{2,1,0:T(8,128)S(1)}, u32[]{:S(2)}, u32[]{:S(2)}) collective-permute-start(f32[1,128,1024]{2,1,0:T(8,128)S(1)} %get-tuple-element.23), channel_id=1, source_target_pairs={{0,1},{1,0},{2,3},{3,2},{4,5},{5,4},{6,7},{7,6},{8,9},{9,8},{10,11... | collective-permute-start | bytes 1572872 | tf_op jit(solution)/shard_map/ppermute | solution.py:37
  28.4 16.5 %collective-permute-start.4 = (f32[1,1,1024]{2,1,0:T(1,128)S(1)}, f32[1,1,1024]{2,1,0:T(1,128)S(1)}, u32[]{:S(2)}, u32[]{:S(2)}) collective-permute-start(f32[1,1,1024]{2,1,0:T(1,128)S(1)} %get-tuple-element.31), channel_id=1, source_target_pairs={{0,8},{8,16},{16,24},{24,32},{32,40},{40,48},{48,56},{56,64},{64,7... | collective-permute-start | bytes 12296 | tf_op jit(solution)/shard_map/ppermute | solution.py:24
  33.7 11.2 %collective-permute-start.5 = (f32[1,1,1024]{2,1,0:T(1,128)S(1)}, f32[1,1,1024]{2,1,0:T(1,128)S(1)}, u32[]{:S(2)}, u32[]{:S(2)}) collective-permute-start(f32[1,1,1024]{2,1,0:T(1,128)S(1)} %get-tuple-element.32), channel_id=1, source_target_pairs={{8,0},{16,8},{24,16},{32,24},{40,32},{48,40},{56,48},{64,56},{72,6... | collective-permute-start | bytes 12296 | tf_op jit(solution)/shard_map/ppermute | solution.py:25
  35.1 5.5 %collective-permute-start.6 = (f32[1,128,1]{2,1,0:T(8,128)S(1)}, f32[1,128,1]{2,1,0:T(8,128)S(1)}, u32[]{:S(2)}, u32[]{:S(2)}) collective-permute-start(f32[1,128,1]{2,1,0:T(8,128)S(1)} %get-tuple-element.29), channel_id=1, source_target_pairs={{0,2},{2,4},{4,6},{1,3},{3,5},{5,7},{8,10},{10,12},{12,14},{9,11},... | collective-permute-start | bytes 1544 | tf_op jit(solution)/shard_map/ppermute | solution.py:24
  38.7 6.2 %collective-permute-start.7 = (f32[1,128,1]{2,1,0:T(8,128)S(1)}, f32[1,128,1]{2,1,0:T(8,128)S(1)}, u32[]{:S(2)}, u32[]{:S(2)}) collective-permute-start(f32[1,128,1]{2,1,0:T(8,128)S(1)} %get-tuple-element.30), channel_id=1, source_target_pairs={{2,0},{4,2},{6,4},{3,1},{5,3},{7,5},{10,8},{12,10},{14,12},{11,9},... | collective-permute-start | bytes 1544 | tf_op jit(solution)/shard_map/ppermute | solution.py:25
  156.4 13.8 %copy-start.2 = (s32[128,1024]{1,0:T(8,128)S(1)}, s32[128,1024]{1,0:T(8,128)}, u32[]{:S(2)}) copy-start(s32[128,1024]{1,0:T(8,128)} %param.9) | copy-start | bytes 1572868
  156.6 13.7 %collective-permute-start.13 = (f32[1,128,1024]{2,1,0:T(8,128)S(1)}, f32[1,128,1024]{2,1,0:T(8,128)S(1)}, u32[]{:S(2)}, u32[]{:S(2)}) collective-permute-start(f32[1,128,1024]{2,1,0:T(8,128)S(1)} %fusion.34), channel_id=1, source_target_pairs={{0,1},{1,0},{2,3},{3,2},{4,5},{5,4},{6,7},{7,6},{8,9},{9,8},{10,11... | collective-permute-start | bytes 1572872 | tf_op jit(solution)/shard_map/ppermute | solution.py:37
  158.7 11.5 %collective-permute-start.9 = (f32[1,1,1024]{2,1,0:T(1,128)S(1)}, f32[1,1,1024]{2,1,0:T(1,128)S(1)}, u32[]{:S(2)}, u32[]{:S(2)}) collective-permute-start(f32[1,1,1024]{2,1,0:T(1,128)S(1)} %get-tuple-element.27), channel_id=1, source_target_pairs={{0,8},{8,16},{16,24},{24,32},{32,40},{40,48},{48,56},{56,64},{64,7... | collective-permute-start | bytes 12296 | tf_op jit(solution)/shard_map/ppermute | solution.py:24
  160.0 10.2 %collective-permute-start.10 = (f32[1,1,1024]{2,1,0:T(1,128)S(1)}, f32[1,1,1024]{2,1,0:T(1,128)S(1)}, u32[]{:S(2)}, u32[]{:S(2)}) collective-permute-start(f32[1,1,1024]{2,1,0:T(1,128)S(1)} %get-tuple-element.28), channel_id=1, source_target_pairs={{8,0},{16,8},{24,16},{32,24},{40,32},{48,40},{56,48},{64,56},{72,6... | collective-permute-start | bytes 12296 | tf_op jit(solution)/shard_map/ppermute | solution.py:25
  161.4 4.5 %collective-permute-start.11 = (f32[1,128,1]{2,1,0:T(8,128)S(1)}, f32[1,128,1]{2,1,0:T(8,128)S(1)}, u32[]{:S(2)}, u32[]{:S(2)}) collective-permute-start(f32[1,128,1]{2,1,0:T(8,128)S(1)} %get-tuple-element.25), channel_id=1, source_target_pairs={{0,2},{2,4},{4,6},{1,3},{3,5},{5,7},{8,10},{10,12},{12,14},{9,11},... | collective-permute-start | bytes 1544 | tf_op jit(solution)/shard_map/ppermute | solution.py:24
  164.1 6.2 %collective-permute-start.12 = (f32[1,128,1]{2,1,0:T(8,128)S(1)}, f32[1,128,1]{2,1,0:T(8,128)S(1)}, u32[]{:S(2)}, u32[]{:S(2)}) collective-permute-start(f32[1,128,1]{2,1,0:T(8,128)S(1)} %get-tuple-element.26), channel_id=1, source_target_pairs={{2,0},{4,2},{6,4},{3,1},{5,3},{7,5},{10,8},{12,10},{14,12},{11,9},... | collective-permute-start | bytes 1544 | tf_op jit(solution)/shard_map/ppermute | solution.py:25
where the time goes:
time: 249 us; the launch traced here: 247 us
  blocking collectives  177 us (71%)
  starting transfers between devices  33 us (13%)
  waiting for transfers between devices  14.6 us (6%)
  other arithmetic  14.5 us (6%)
  between operations  6.6 us (3%)
    psum x6, blocking collectives, over_axes(): return functools.reduce(lax.psum, axes, value)  177 us
    ppermute x6, starting transfers between devices, with_halo(): lax.ppermute(last, axis, up)  21.1 us
    ppermute x6, waiting for transfers between devices, with_halo(): lax.ppermute(initial, axis, [(b, a) for a, b in up])  12.9 us
    ppermute x6, starting transfers between devices, with_halo(): lax.ppermute(initial, axis, [(b, a) for a, b in up])  7.85 us
    add x1, other arithmetic, lookup(): cond + jnp.where(node_class == klass, class_conductance[:, klass][:, None...  6.57 us
  transfers between devices with their start and end apart: 14, of which 6 were waited for; matrix products, arithmetic and copies ran while one was open for 0% of the time, Pallas kernels for 0%

commit v1 on v0

--- a/solution.py
+++ b/solution.py
@@ -4,8 +4,6 @@
 import jax.numpy as jnp
 from jax import lax
 from jax.sharding import PartitionSpec as P
-
-ITERS = 2
 
 
 via_conductance = 2.0
@@ -84,33 +82,31 @@
         + pad_conductance * pad_mask.astype(jnp.float32)
         + leakage
     )
-    drop_field = jnp.zeros_like(current)
-    resid = current
-    worst_field = drop_field
-
-    def inner_pair(resid_now):
-        precond_now = resid_now / diagonal
-        image_now = apply_grid(precond_now, edges, diagonal, coupling)
-        energy_part, curve_part = (
-            over_axes(jnp.sum(resid_now * precond_now), ("row", "col", "layer")),
-            over_axes(jnp.sum(precond_now * image_now), ("row", "col", "layer")),
-        )
-        return (precond_now, image_now, energy_part, curve_part)
-
-    precond, image, energy_now, curve_now = inner_pair(resid)
-    step_size = energy_now / curve_now
-    direction, along = (precond, image)
-    for iteration in range(ITERS):
-        drop_field = drop_field + step_size * direction
-        resid = resid - step_size * along
-        worst_field = drop_field if iteration == 0 else jnp.maximum(worst_field, drop_field)
-        if iteration + 1 < ITERS:
-            precond, image, energy_next, curve_now = inner_pair(resid)
-            ratio = energy_next / energy_now
-            step_size = energy_next / (curve_now - ratio * energy_next / step_size)
-            direction = precond + ratio * direction
-            along = image + ratio * along
-            energy_now = energy_next
+    precond = current / diagonal
+    image = apply_grid(precond, edges, diagonal, coupling)
+    second = image / diagonal
+    second_image = apply_grid(second, edges, diagonal, coupling)
+    sums = jnp.stack(
+        [
+            jnp.sum(current * precond),
+            jnp.sum(precond * image),
+            jnp.sum(image * second),
+            jnp.sum(second * second_image),
+        ]
+    )
+    sums = over_axes(sums, ("layer", "col", "row"))
+    first_step = sums[0] / sums[1]
+    ratio = sums[0] * sums[2] / (sums[1] * sums[1]) - 1.0
+    energy = ratio * sums[0]
+    grown = 1.0 + ratio
+    curve = grown * grown * sums[1] - 2.0 * first_step * grown * sums[2]
+    curve = curve + first_step * first_step * sums[3]
+    second_step = energy / curve
+    along = first_step + second_step * grown
+    back = first_step * second_step
+    drop_field = along * precond - back * second
+    resid = current - along * image + back * second_image
+    worst_field = jnp.maximum(first_step * precond, drop_field)
     return (drop_field, resid, worst_field)
 
 

time: 249 us -> 182 us (0.73)
  blocking collectives: 177 us -> 105 us
  starting transfers between devices: 33 us -> 37.6 us
    psum x6 -> x3, blocking collectives: 177 us -> 105 us  [over_axes(): return functools.reduce(lax.psum, axes, value)]
    ppermute x6, starting transfers between devices: 21.1 us -> 25.8 us  [with_halo(): lax.ppermute(last, axis, up)]
    another operation x0 -> x1, other arithmetic: none -> 2.57 us  [local(): jnp.stack([jnp.sum(current * precond), jnp.sum(precond * image), jnp.sum(...]
where the time goes in v1:
time: 182 us; the launch traced here: 181 us
  blocking collectives  105 us (58%)
  starting transfers between devices  37.6 us (21%)
  waiting for transfers between devices  14.6 us (8%)
  other arithmetic  14.5 us (8%)
  between operations  7.14 us (4%)
  local copies, waits for them, and re-layouts  2.5 us (1%)
    psum x3, blocking collectives, over_axes(): return functools.reduce(lax.psum, axes, value)  105 us
    ppermute x6, starting transfers between devices, with_halo(): lax.ppermute(last, axis, up)  25.8 us
    ppermute x6, waiting for transfers between devices, with_halo(): lax.ppermute(initial, axis, [(b, a) for a, b in up])  12.9 us
    ppermute x6, starting transfers between devices, with_halo(): lax.ppermute(initial, axis, [(b, a) for a, b in up])  7.85 us
    add x1, other arithmetic, lookup(): cond + jnp.where(node_class == klass, class_conductance[:, klass][:, None...  6.58 us
    ppermute x2, starting transfers between devices, from_partner(): lax.ppermute(value, axis, [(i, i ^ 1 << stride) for i in range(lax.axis_s...  3.9 us
  transfers between devices with their start and end apart: 14, of which 6 were waited for; matrix products, arithmetic and copies ran while one was open for 0% of the time, Pallas kernels for 0%

profile of v1, /device:TPU:40, one launch (start us, length us, event | category | flops | bytes accessed | tf_op | source)
XLA Modules:
  0.0 181.1 jit_solution(9709911372553833029)
XLA Ops:
  0.6 1.6 fusion.46
  2.2 0.0 copy-start
  2.3 0.0 copy-start.1
  2.3 6.6 %select_add_fusion = f32[1,128,1024]{2,1,0:T(8,128)S(1)} fusion(s32[1,128,1024]{2,1,0:T(8,128)} %param.6, f32[]{:T(128)} %bitcast.7, f32[]{:T(128)} %bitcast.6, f32[]{:T(128)} %bitcast.5, f32[]{:T(128)} %bitcast.4, f32[]{:T(128)} %bitcast.3, f32[]{:T(128)} %bitcast.2, f32[]{:T(128)} %bitcast.1, f32[]{:T(128)} %bitcast), kind=kLoop, calls=%fused_computation.73 | loop fusion | flops 3014656 | bytes 1048608 | tf_op jit(solution)/shard_map/add | solution.py:45
  8.9 4.7 %collective-permute-start = (f32[1,1,1024]{2,1,0:T(1,128)S(1)}, f32[1,1,1024]{2,1,0:T(1,128)S(1)}, u32[]{:S(2)}, u32[]{:S(2)}) collective-permute-start(f32[1,1,1024]{2,1,0:T(1,128)S(1)} %get-tuple-element.24), channel_id=1, source_target_pairs={{0,8},{8,16},{16,24},{24,32},{32,40},{40,48},{48,56},{56,64},{64,7... | collective-permute-start | bytes 12296 | tf_op jit(solution)/shard_map/ppermute | solution.py:22
  13.6 1.3 collective-permute-start.1
  14.9 0.1 fusion.43
  15.0 3.6 %collective-permute-start.2 = (f32[1,128,1]{2,1,0:T(8,128)S(1)}, f32[1,128,1]{2,1,0:T(8,128)S(1)}, u32[]{:S(2)}, u32[]{:S(2)}) collective-permute-start(f32[1,128,1]{2,1,0:T(8,128)S(1)} %get-tuple-element.22), channel_id=1, source_target_pairs={{0,2},{2,4},{4,6},{1,3},{3,5},{5,7},{8,10},{10,12},{12,14},{9,11},... | collective-permute-start | bytes 1544 | tf_op jit(solution)/shard_map/ppermute | solution.py:22
  18.5 1.3 collective-permute-start.3
  19.9 0.6 collective-permute-done.2
  20.4 4.3 %collective-permute-done.3 = f32[1,128,1]{2,1,0:T(8,128)S(1)} collective-permute-done((f32[1,128,1]{2,1,0:T(8,128)S(1)}, f32[1,128,1]{2,1,0:T(8,128)S(1)}, u32[]{:S(2)}, u32[]{:S(2)}) %collective-permute-start.3) | collective-permute-done | bytes 544 | tf_op jit(solution)/shard_map/ppermute | solution.py:23
  24.7 0.0 collective-permute-done
  24.7 0.0 collective-permute-done.1
  24.7 0.0 copy-done
  24.7 0.0 copy-done.1
  24.8 1.7 fusion.37
  26.4 2.0 %collective-permute-start.8 = (f32[1,128,1024]{2,1,0:T(8,128)S(1)}, f32[1,128,1024]{2,1,0:T(8,128)S(1)}, u32[]{:S(2)}, u32[]{:S(2)}) collective-permute-start(f32[1,128,1024]{2,1,0:T(8,128)S(1)} %get-tuple-element.12), channel_id=1, source_target_pairs={{0,1},{1,0},{2,3},{3,2},{4,5},{5,4},{6,7},{7,6},{8,9},{9,8},{10,11... | collective-permute-start | bytes 1572872 | tf_op jit(solution)/shard_map/ppermute | solution.py:35
  28.4 5.4 %collective-permute-start.4 = (f32[1,1,1024]{2,1,0:T(1,128)S(1)}, f32[1,1,1024]{2,1,0:T(1,128)S(1)}, u32[]{:S(2)}, u32[]{:S(2)}) collective-permute-start(f32[1,1,1024]{2,1,0:T(1,128)S(1)} %get-tuple-element.20), channel_id=1, source_target_pairs={{0,8},{8,16},{16,24},{24,32},{32,40},{40,48},{48,56},{56,64},{64,7... | collective-permute-start | bytes 12296 | tf_op jit(solution)/shard_map/ppermute | solution.py:22
  33.8 1.3 collective-permute-start.5
  35.1 0.1 fusion.41
  35.2 3.6 %collective-permute-start.6 = (f32[1,128,1]{2,1,0:T(8,128)S(1)}, f32[1,128,1]{2,1,0:T(8,128)S(1)}, u32[]{:S(2)}, u32[]{:S(2)}) collective-permute-start(f32[1,128,1]{2,1,0:T(8,128)S(1)} %get-tuple-element.18), channel_id=1, source_target_pairs={{0,2},{2,4},{4,6},{1,3},{3,5},{5,7},{8,10},{10,12},{12,14},{9,11},... | collective-permute-start | bytes 1544 | tf_op jit(solution)/shard_map/ppermute | solution.py:22
  38.7 1.3 collective-permute-start.7
  40.0 0.6 collective-permute-done.6
  40.6 4.3 %collective-permute-done.7 = f32[1,128,1]{2,1,0:T(8,128)S(1)} collective-permute-done((f32[1,128,1]{2,1,0:T(8,128)S(1)}, f32[1,128,1]{2,1,0:T(8,128)S(1)}, u32[]{:S(2)}, u32[]{:S(2)}) %collective-permute-start.7) | collective-permute-done | bytes 544 | tf_op jit(solution)/shard_map/ppermute | solution.py:23
  44.9 0.0 collective-permute-done.4
  44.9 0.0 collective-permute-done.5
  44.9 0.0 collective-permute-done.8
  44.9 0.8 fusion.35
  45.8 2.0 %collective-permute-start.13 = (f32[1,128,1024]{2,1,0:T(8,128)S(1)}, f32[1,128,1024]{2,1,0:T(8,128)S(1)}, u32[]{:S(2)}, u32[]{:S(2)}) collective-permute-start(f32[1,128,1024]{2,1,0:T(8,128)S(1)} %get-tuple-element.10), channel_id=1, source_target_pairs={{0,1},{1,0},{2,3},{3,2},{4,5},{5,4},{6,7},{7,6},{8,9},{9,8},{10,11... | collective-permute-start | bytes 1572872 | tf_op jit(solution)/shard_map/ppermute | solution.py:35
  47.8 5.4 %collective-permute-start.9 = (f32[1,1,1024]{2,1,0:T(1,128)S(1)}, f32[1,1,1024]{2,1,0:T(1,128)S(1)}, u32[]{:S(2)}, u32[]{:S(2)}) collective-permute-start(f32[1,1,1024]{2,1,0:T(1,128)S(1)} %get-tuple-element.16), channel_id=1, source_target_pairs={{0,8},{8,16},{16,24},{24,32},{32,40},{40,48},{48,56},{56,64},{64,7... | collective-permute-start | bytes 12296 | tf_op jit(solution)/shard_map/ppermute | solution.py:22
  53.1 1.3 collective-permute-start.10
  54.4 0.1 fusion.39
  54.5 3.3 %collective-permute-start.11 = (f32[1,128,1]{2,1,0:T(8,128)S(1)}, f32[1,128,1]{2,1,0:T(8,128)S(1)}, u32[]{:S(2)}, u32[]{:S(2)}) collective-permute-start(f32[1,128,1]{2,1,0:T(8,128)S(1)} %get-tuple-element.14), channel_id=1, source_target_pairs={{0,2},{2,4},{4,6},{1,3},{3,5},{5,7},{8,10},{10,12},{12,14},{9,11},... | collective-permute-start | bytes 1544 | tf_op jit(solution)/shard_map/ppermute | solution.py:22
  57.8 1.3 collective-permute-start.12
  59.1 0.6 collective-permute-done.11
  59.7 4.3 %collective-permute-done.12 = f32[1,128,1]{2,1,0:T(8,128)S(1)} collective-permute-done((f32[1,128,1]{2,1,0:T(8,128)S(1)}, f32[1,128,1]{2,1,0:T(8,128)S(1)}, u32[]{:S(2)}, u32[]{:S(2)}) %collective-permute-start.12) | collective-permute-done | bytes 544 | tf_op jit(solution)/shard_map/ppermute | solution.py:23
  64.0 0.0 collective-permute-done.9
  64.0 0.0 collective-permute-done.10
  64.0 0.0 collective-permute-done.13
  64.0 1.5 multiply_reduce_fusion.3
  65.5 2.6 %pad_maximum_fusion.18 = f32[4]{0:T(128)S(1)} fusion(f32[1]{0:T(128)} %bitcast.12, f32[1]{0:T(128)} %bitcast.11, f32[1]{0:T(128)} %bitcast.10, f32[1]{0:T(128)} %bitcast.9), kind=kLoop, calls=%fused_computation.74 | loop fusion | flops 12 | bytes 32 | tf_op jit(solution)/shard_map/stack | solution.py:89
  68.1 2.5 %psum.21 = f32[4]{0:T(128)S(1)} all-reduce(f32[4]{0:T(128)S(1)} %pad_maximum_fusion.18), channel_id=1, replica_groups=mesh['scen'=2,'row'=32,'col'=4,'layer'=2] {'layer'}, use_global_device_ids=true, to_apply=%region_4.5 | all-reduce | flops 4 | bytes 32 | tf_op jit(solution)/shard_map/psum | solution.py:39
  70.6 7.8 %psum.22 = f32[4]{0:T(128)S(1)} all-reduce(f32[4]{0:T(128)S(1)} %psum.21), channel_id=1, replica_groups=mesh['scen'=2,'row'=32,'col'=4,'layer'=2] {'col'}, use_global_device_ids=true, to_apply=%region_5.6 | all-reduce | flops 4 | bytes 32 | tf_op jit(solution)/shard_map/psum | solution.py:39
  78.4 94.5 %psum.23 = f32[4]{0:T(128)S(1)} all-reduce(f32[4]{0:T(128)S(1)} %psum.22), channel_id=1, replica_groups=mesh['scen'=2,'row'=32,'col'=4,'layer'=2] {'row'}, use_global_device_ids=true, to_apply=%region_6.7 | all-reduce | flops 4 | bytes 32 | tf_op jit(solution)/shard_map/psum | solution.py:39
  172.9 0.6 fusion.45
  179.8 1.3 multiply_maximum_fusion
  (3 shorter events, 0.0 us)
Async XLA Ops:
  2.2 22.5 %copy-start = (s32[128,1024]{1,0:T(8,128)S(1)}, s32[128,1024]{1,0:T(8,128)}, u32[]{:S(2)}) copy-start(s32[128,1024]{1,0:T(8,128)} %param.9) | copy-start | bytes 1572868
  2.3 22.5 %copy-start.1 = (f32[1,128,1024]{2,1,0:T(8,128)S(1)}, f32[1,128,1024]{2,1,0:T(8,128)}, u32[]{:S(2)}) copy-start(f32[1,128,1024]{2,1,0:T(8,128)} %param.5) | copy-start | bytes 1572868
  8.9 15.9 %collective-permute-start = (f32[1,1,1024]{2,1,0:T(1,128)S(1)}, f32[1,1,1024]{2,1,0:T(1,128)S(1)}, u32[]{:S(2)}, u32[]{:S(2)}) collective-permute-start(f32[1,1,1024]{2,1,0:T(1,128)S(1)} %get-tuple-element.24), channel_id=1, source_target_pairs={{0,8},{8,16},{16,24},{24,32},{32,40},{40,48},{48,56},{56,64},{64,7... | collective-permute-start | bytes 12296 | tf_op jit(solution)/shard_map/ppermute | solution.py:22
  13.6 11.2 %collective-permute-start.1 = (f32[1,1,1024]{2,1,0:T(1,128)S(1)}, f32[1,1,1024]{2,1,0:T(1,128)S(1)}, u32[]{:S(2)}, u32[]{:S(2)}) collective-permute-start(f32[1,1,1024]{2,1,0:T(1,128)S(1)} %get-tuple-element.25), channel_id=1, source_target_pairs={{8,0},{16,8},{24,16},{32,24},{40,32},{48,40},{56,48},{64,56},{72,6... | collective-permute-start | bytes 12296 | tf_op jit(solution)/shard_map/ppermute | solution.py:23
  15.0 5.5 %collective-permute-start.2 = (f32[1,128,1]{2,1,0:T(8,128)S(1)}, f32[1,128,1]{2,1,0:T(8,128)S(1)}, u32[]{:S(2)}, u32[]{:S(2)}) collective-permute-start(f32[1,128,1]{2,1,0:T(8,128)S(1)} %get-tuple-element.22), channel_id=1, source_target_pairs={{0,2},{2,4},{4,6},{1,3},{3,5},{5,7},{8,10},{10,12},{12,14},{9,11},... | collective-permute-start | bytes 1544 | tf_op jit(solution)/shard_map/ppermute | solution.py:22
  18.5 6.2 %collective-permute-start.3 = (f32[1,128,1]{2,1,0:T(8,128)S(1)}, f32[1,128,1]{2,1,0:T(8,128)S(1)}, u32[]{:S(2)}, u32[]{:S(2)}) collective-permute-start(f32[1,128,1]{2,1,0:T(8,128)S(1)} %get-tuple-element.23), channel_id=1, source_target_pairs={{2,0},{4,2},{6,4},{3,1},{5,3},{7,5},{10,8},{12,10},{14,12},{11,9},... | collective-permute-start | bytes 1544 | tf_op jit(solution)/shard_map/ppermute | solution.py:23
  26.4 18.5 %collective-permute-start.8 = (f32[1,128,1024]{2,1,0:T(8,128)S(1)}, f32[1,128,1024]{2,1,0:T(8,128)S(1)}, u32[]{:S(2)}, u32[]{:S(2)}) collective-permute-start(f32[1,128,1024]{2,1,0:T(8,128)S(1)} %get-tuple-element.12), channel_id=1, source_target_pairs={{0,1},{1,0},{2,3},{3,2},{4,5},{5,4},{6,7},{7,6},{8,9},{9,8},{10,11... | collective-permute-start | bytes 1572872 | tf_op jit(solution)/shard_map/ppermute | solution.py:35
  28.4 16.5 %collective-permute-start.4 = (f32[1,1,1024]{2,1,0:T(1,128)S(1)}, f32[1,1,1024]{2,1,0:T(1,128)S(1)}, u32[]{:S(2)}, u32[]{:S(2)}) collective-permute-start(f32[1,1,1024]{2,1,0:T(1,128)S(1)} %get-tuple-element.20), channel_id=1, source_target_pairs={{0,8},{8,16},{16,24},{24,32},{32,40},{40,48},{48,56},{56,64},{64,7... | collective-permute-start | bytes 12296 | tf_op jit(solution)/shard_map/ppermute | solution.py:22
  33.8 11.2 %collective-permute-start.5 = (f32[1,1,1024]{2,1,0:T(1,128)S(1)}, f32[1,1,1024]{2,1,0:T(1,128)S(1)}, u32[]{:S(2)}, u32[]{:S(2)}) collective-permute-start(f32[1,1,1024]{2,1,0:T(1,128)S(1)} %get-tuple-element.21), channel_id=1, source_target_pairs={{8,0},{16,8},{24,16},{32,24},{40,32},{48,40},{56,48},{64,56},{72,6... | collective-permute-start | bytes 12296 | tf_op jit(solution)/shard_map/ppermute | solution.py:23
  35.2 5.5 %collective-permute-start.6 = (f32[1,128,1]{2,1,0:T(8,128)S(1)}, f32[1,128,1]{2,1,0:T(8,128)S(1)}, u32[]{:S(2)}, u32[]{:S(2)}) collective-permute-start(f32[1,128,1]{2,1,0:T(8,128)S(1)} %get-tuple-element.18), channel_id=1, source_target_pairs={{0,2},{2,4},{4,6},{1,3},{3,5},{5,7},{8,10},{10,12},{12,14},{9,11},... | collective-permute-start | bytes 1544 | tf_op jit(solution)/shard_map/ppermute | solution.py:22
  38.7 6.2 %collective-permute-start.7 = (f32[1,128,1]{2,1,0:T(8,128)S(1)}, f32[1,128,1]{2,1,0:T(8,128)S(1)}, u32[]{:S(2)}, u32[]{:S(2)}) collective-permute-start(f32[1,128,1]{2,1,0:T(8,128)S(1)} %get-tuple-element.19), channel_id=1, source_target_pairs={{2,0},{4,2},{6,4},{3,1},{5,3},{7,5},{10,8},{12,10},{14,12},{11,9},... | collective-permute-start | bytes 1544 | tf_op jit(solution)/shard_map/ppermute | solution.py:23
  45.8 18.2 %collective-permute-start.13 = (f32[1,128,1024]{2,1,0:T(8,128)S(1)}, f32[1,128,1024]{2,1,0:T(8,128)S(1)}, u32[]{:S(2)}, u32[]{:S(2)}) collective-permute-start(f32[1,128,1024]{2,1,0:T(8,128)S(1)} %get-tuple-element.10), channel_id=1, source_target_pairs={{0,1},{1,0},{2,3},{3,2},{4,5},{5,4},{6,7},{7,6},{8,9},{9,8},{10,11... | collective-permute-start | bytes 1572872 | tf_op jit(solution)/shard_map/ppermute | solution.py:35
  47.8 16.2 %collective-permute-start.9 = (f32[1,1,1024]{2,1,0:T(1,128)S(1)}, f32[1,1,1024]{2,1,0:T(1,128)S(1)}, u32[]{:S(2)}, u32[]{:S(2)}) collective-permute-start(f32[1,1,1024]{2,1,0:T(1,128)S(1)} %get-tuple-element.16), channel_id=1, source_target_pairs={{0,8},{8,16},{16,24},{24,32},{32,40},{40,48},{48,56},{56,64},{64,7... | collective-permute-start | bytes 12296 | tf_op jit(solution)/shard_map/ppermute | solution.py:22
  53.1 10.9 %collective-permute-start.10 = (f32[1,1,1024]{2,1,0:T(1,128)S(1)}, f32[1,1,1024]{2,1,0:T(1,128)S(1)}, u32[]{:S(2)}, u32[]{:S(2)}) collective-permute-start(f32[1,1,1024]{2,1,0:T(1,128)S(1)} %get-tuple-element.17), channel_id=1, source_target_pairs={{8,0},{16,8},{24,16},{32,24},{40,32},{48,40},{56,48},{64,56},{72,6... | collective-permute-start | bytes 12296 | tf_op jit(solution)/shard_map/ppermute | solution.py:23
  54.5 5.2 %collective-permute-start.11 = (f32[1,128,1]{2,1,0:T(8,128)S(1)}, f32[1,128,1]{2,1,0:T(8,128)S(1)}, u32[]{:S(2)}, u32[]{:S(2)}) collective-permute-start(f32[1,128,1]{2,1,0:T(8,128)S(1)} %get-tuple-element.14), channel_id=1, source_target_pairs={{0,2},{2,4},{4,6},{1,3},{3,5},{5,7},{8,10},{10,12},{12,14},{9,11},... | collective-permute-start | bytes 1544 | tf_op jit(solution)/shard_map/ppermute | solution.py:22
  57.8 6.2 %collective-permute-start.12 = (f32[1,128,1]{2,1,0:T(8,128)S(1)}, f32[1,128,1]{2,1,0:T(8,128)S(1)}, u32[]{:S(2)}, u32[]{:S(2)}) collective-permute-start(f32[1,128,1]{2,1,0:T(8,128)S(1)} %get-tuple-element.15), channel_id=1, source_target_pairs={{2,0},{4,2},{6,4},{3,1},{5,3},{7,5},{10,8},{12,10},{14,12},{11,9},... | collective-permute-start | bytes 1544 | tf_op jit(solution)/shard_map/ppermute | solution.py:23

commit v2 on v1

v2 whole, which is shorter than its diff:
```python
import functools

import jax
import jax.numpy as jnp
from jax import lax
from jax.experimental import pallas as pl
from jax.experimental.pallas import tpu as pltpu
from jax.sharding import PartitionSpec as P

MESH = pl.DeviceIdType.MESH

via_conductance = 2.0
pad_conductance = 4.0
leakage = 0.05

S0, S1, Q0, Q1, Q2, E0, E1, E2, GUESS = range(9)


def lanes_of(shape):
    return lax.broadcasted_iota(jnp.int32, shape, len(shape) - 1)


def rows_of(shape):
    return lax.broadcasted_iota(jnp.int32, shape, len(shape) - 2)


def pick(record, lane, axis=None):
    kept = jnp.where(lanes_of(record.shape) == lane, record, 0.0)
    return jnp.sum(kept, axis=axis, keepdims=True)


def by_lane(shape, entries):
    lane = lanes_of(shape)
    out = jnp.zeros(shape, jnp.float32)
    for where, value in entries:
        out = jnp.where(lane == where, value, out)
    return out


def fold(value):
    parts = [value[:, i : i + 128] for i in range(0, value.shape[1], 128)]
    while len(parts) > 1:
        parts = [a + b for a, b in zip(parts[::2], parts[1::2])]
    return parts[0]


def kernel(
    nz,
    nx,
    nc,
    cur_hbm,
    cls_hbm,
    cc_ref,
    pad_hbm,
    via_hbm,
    z_hbm,
    w_hbm,
    y_hbm,
    u_hbm,
    scal_ref,
    cur,
    cls,
    pad,
    via,
    cond_p,
    z_p,
    y_p,
    inv,
    w,
    u,
    zother,
    yother,
    srow,
    scol,
    rrow,
    rcol,
    srec,
    plane,
    zrec,
    zbuf,
    in_sem,
    out_sem,
    halo_ssem,
    halo_rsem,
    other_ssem,
    other_rsem,
    plane_ssem,
    plane_rsem,
    z_ssem,
    z_rsem,
    ready,
):
    iz, ix, ic = lax.axis_index("row"), lax.axis_index("col"), lax.axis_index("layer")
    rows, cols = cur.shape
    chunks = rows // 8
    np_ = nx * nc
    me = ix * nc + ic

    loads = [
        pltpu.make_async_copy(src, dst, in_sem.at[i])
        for i, (src, dst) in enumerate(
            ((cls_hbm, cls), (cur_hbm, cur), (pad_hbm, pad), (via_hbm, via))
        )
    ]
    for copy in loads:
        copy.start()

    rrow[...] = jnp.zeros(rrow.shape, jnp.float32)
    rcol[...] = jnp.zeros(rcol.shape, jnp.float32)

    barrier = pltpu.get_barrier_semaphore()
    zup, zdown = lax.rem(iz + nz - 1, nz), lax.rem(iz + 1, nz)
    for near in (zup, zdown):
        pl.semaphore_signal(barrier, inc=1, device_id={"row": near}, device_id_type=MESH)

    def plane_peer(step):
        other = lax.rem(me + step, np_)
        return {"col": other // nc, "layer": lax.rem(other, nc)}

    for step in range(1, np_):
        pl.semaphore_signal(barrier, inc=1, device_id=plane_peer(step), device_id_type=MESH)
    pl.semaphore_wait(barrier, np_ + 1)

    levels = (nz // 2).bit_length() - 1

    def greet(level):
        if level >= levels:
            return
        far = 1 << level
        for near in (lax.rem(iz + far, nz), lax.rem(iz + nz - far, nz)):
            pl.semaphore_signal(
                ready.at[level], inc=1, device_id={"row": near}, device_id_type=MESH
            )

    def greeted(level):
        if level < levels:
            pl.semaphore_wait(ready.at[level], 2)

    greet(0)

    sides = (
        (srow, rrow, 0, 1, iz > 0, iz < nz - 1, {"row": iz - 1}),
        (srow, rrow, 1, 0, iz < nz - 1, iz > 0, {"row": iz + 1}),
        (scol, rcol, 0, 1, ix > 0, ix < nx - 1, {"col": ix - 1}),
        (scol, rcol, 1, 0, ix < nx - 1, ix > 0, {"col": ix + 1}),
    )

    def halo(turn, i):
        src, dst, mine, theirs, _, _, target = sides[i]
        return pltpu.make_async_remote_copy(
            src_ref=src.at[turn, mine],
            dst_ref=dst.at[turn, theirs],
            send_sem=halo_ssem.at[turn, i],
            recv_sem=halo_rsem.at[turn, i],
            device_id=target,
            device_id_type=MESH,
        )

    def send_halo(turn, field, left, right):
        srow[turn, 0] = field[8:9, :]
        srow[turn, 1] = field[rows + 7 : rows + 8, :]
        scol[turn, 0] = left
        scol[turn, 1] = right
        for i in range(4):
            pl.when(sides[i][4])(halo(turn, i).start)

    def take_halo(turn, field):
        for i in range(4):
            pl.when(sides[i][5])(halo(turn, i).wait_recv)
        field[0:8, :] = jnp.broadcast_to(rrow[turn, 0], (8, cols))
        field[rows + 8 : rows + 16, :] = jnp.broadcast_to(rrow[turn, 1], (8, cols))

    def end_halo(turn):
        for i in range(4):
            pl.when(sides[i][4])(halo(turn, i).wait_send)

    def to_other(turn, src, dst):
        return pltpu.make_async_remote_copy(
            src_ref=src.at[pl.ds(8, rows)],
            dst_ref=dst,
            send_sem=other_ssem.at[turn],
            recv_sem=other_rsem.at[turn],
            device_id={"layer": 1 - ic},
            device_id_type=MESH,
        )

    tile = (8, cols)
    block = (8, 128)
    zero = jnp.zeros(block, jnp.float32)
    sub = rows_of(tile)
    narrow_lane = lanes_of(block)

    def at(k, shift=0):
        return pl.ds(pl.multiple_of(8 * k + shift, 8), 8)

    def packed(k, value, left, right):
        here = narrow_lane == k
        left = jnp.where(here, pltpu.roll(value[:, :128], k, 1), left)
        right = jnp.where(here, pltpu.roll(value[:, cols - 128 :], k + 1, 1), right)
        return left, right

    def around(k, prev, here, after, left, right):
        up = pltpu.roll(jnp.where(sub == 7, prev, here), 1, 0)
        down = pltpu.roll(jnp.where(sub == 0, after, here), 7, 0)
        left = pltpu.roll(left, lax.rem(128 - k, 128), 1)
        right = pltpu.roll(right, 127 - k, 1)
        west = pltpu.roll(here, 1, 1)
        west = jnp.concatenate(
            [jnp.where(narrow_lane == 0, left, west[:, :128]), west[:, 128:]], axis=1
        )
        east = pltpu.roll(here, cols - 1, 1)
        east = jnp.concatenate(
            [
                east[:, : cols - 128],
                jnp.where(narrow_lane == 127, right, east[:, cols - 128 :]),
            ],
            axis=1,
        )
        return (up + down) + (west + east)

    loads[0].wait()

    def look_up(k, carry):
        klass = cls[at(k), :]
        level = [cc_ref[0, i] for i in range(8)]
        for bit in range(3):
            high = (klass & (1 << bit)) != 0
            level = [jnp.where(high, b, a) for a, b in zip(level[::2], level[1::2])]
        cond_p[at(k, 8), :] = level[0]
        return packed(k, level[0], *carry)

    left, right = lax.fori_loop(0, chunks, look_up, (zero, zero))
    send_halo(0, cond_p, left, right)
    greeted(0)
    greet(1)
    for copy in loads[1:]:
        copy.wait()
    take_halo(0, cond_p)

    lane = lanes_of(tile)
    one = jnp.float32(1.0)
    beside_x = 4.0 - jnp.where((lane == 0) & (ix == 0), one, 0.0)
    beside_x = beside_x - jnp.where((lane == cols - 1) & (ix == nx - 1), one, 0.0)
    cond_left, cond_right = rcol[0, 0], rcol[0, 1]

    def precondition(k, carry):
        left, right, energy = carry
        here = cond_p[at(k, 8), :]
        near = around(
            k, cond_p[at(k), :], here, cond_p[at(k, 16), :], cond_left, cond_right
        )
        row = sub + 8 * k
        beside = beside_x - jnp.where((row == 0) & (iz == 0), one, 0.0)
        beside = beside - jnp.where((row == rows - 1) & (iz == nz - 1), one, 0.0)
        diagonal = 0.5 * (beside * here + near)
        diagonal = diagonal + via_conductance * via[at(k), :].astype(jnp.float32)
        diagonal = diagonal + (
            pad_conductance * pad[at(k), :].astype(jnp.float32) + leakage
        )
        inverse = 1.0 / diagonal
        resid = cur[at(k), :]
        value = resid * inverse
        inv[at(k), :] = inverse
        z_p[at(k, 8), :] = value
        left, right = packed(k, value, left, right)
        return left, right, energy + fold(resid * value)

    left, right, energy = lax.fori_loop(0, chunks, precondition, (zero, zero, zero))
    to_other(0, z_p, zother).start()
    send_halo(1, z_p, left, right)
    greeted(1)
    greet(2)
    save_z = pltpu.make_async_copy(z_p.at[pl.ds(8, rows)], z_hbm, out_sem.at[0])
    save_z.start()
    take_halo(1, z_p)
    to_other(0, z_p, zother).wait_recv()

    def image(k, field, lead, left, right, other):
        conds = [cond_p[at(k, 8 * i), :] for i in range(3)]
        values = [field[at(k, 8 * i), :] for i in range(3)]
        flux = [a * b for a, b in zip(conds, values)]
        plain = around(k, *values, left, right)
        scaled = around(k, *flux, cond_left * left, cond_right * right)
        across = via_conductance * via[at(k), :].astype(jnp.float32) * other[at(k), :]
        return lead - 0.5 * (conds[1] * plain + scaled) - across, values[1]

    z_left, z_right = rcol[1, 0], rcol[1, 1]

    def first_image(k, carry):
        left, right, curve = carry
        out, value = image(k, z_p, cur[at(k), :], z_left, z_right, zother)
        w[at(k), :] = out
        nxt = out * inv[at(k), :]
        y_p[at(k, 8), :] = nxt
        left, right = packed(k, nxt, left, right)
        return left, right, curve + fold(value * out)

    left, right, curve = lax.fori_loop(0, chunks, first_image, (zero, zero, zero))
    to_other(1, y_p, yother).start()
    send_halo(2, y_p, left, right)
    greeted(2)
    greet(3)
    save_w = pltpu.make_async_copy(w, w_hbm, out_sem.at[1])
    save_w.start()
    save_y = pltpu.make_async_copy(y_p.at[pl.ds(8, rows)], y_hbm, out_sem.at[2])
    save_y.start()
    energy = jnp.sum(energy, keepdims=True)
    curve = jnp.sum(curve, keepdims=True)
    guess = energy / curve
    take_halo(2, y_p)
    to_other(1, y_p, yother).wait_recv()

    y_left, y_right = rcol[2, 0], rcol[2, 1]

    def second_image(k, sums):
        along = w[at(k), :]
        out, nxt = image(k, y_p, along, y_left, y_right, yother)
        u[at(k), :] = out
        left_over = cur[at(k), :] - guess * along
        pre = left_over * inv[at(k), :]
        pre_image = along - guess * out
        terms = (
            left_over * pre,
            left_over * nxt,
            along * nxt,
            pre * pre_image,
            pre * out + nxt * pre_image,
            nxt * out,
        )
        return tuple(a + fold(b) for a, b in zip(sums, terms))

    sums = lax.fori_loop(0, chunks, second_image, (zero,) * 6)
    save_u = pltpu.make_async_copy(u, u_hbm, out_sem.at[3])
    save_u.start()

    line = (1, 128)
    entries = [(S0, energy), (S1, curve), (GUESS, guess)]
    entries += [
        (spot, jnp.sum(value, keepdims=True))
        for spot, value in zip((Q0, Q1, Q2, E0, E1, E2), sums)
    ]
    record = by_lane(line, entries)
    srec[...] = record
    plane[me] = record

    def in_plane(step):
        return pltpu.make_async_remote_copy(
            src_ref=srec,
            dst_ref=plane.at[me],
            send_sem=plane_ssem.at[step],
            recv_sem=plane_rsem.at[step],
            device_id=plane_peer(step),
            device_id_type=MESH,
        )

    for step in range(1, np_):
        in_plane(step).start()
    for step in range(1, np_):
        in_plane(step).wait_recv()

    records = plane[...].reshape(np_, 128)
    joint = pick(records, S0) / pick(records, S1)
    delta = joint - pick(records, GUESS, axis=1)
    first = by_lane(
        records.shape,
        [(Q0, -2.0 * delta), (Q1, -delta), (E0, -delta), (E1, -2.0 * delta)],
    )
    second = by_lane(records.shape, [(Q0, delta * delta), (E0, delta * delta)])
    records = (
        records
        + first * pltpu.roll(records, 127, 1)
        + second * pltpu.roll(records, 126, 1)
    )
    record = jnp.sum(records, axis=0, keepdims=True)
    record = jnp.where(lanes_of(line) == GUESS, joint, record)
    zrec[...] = record
    zbuf[iz] = record
    greeted(3)

    def along_z(i):
        away = (i + 1) // 2
        step = nz // 2 + away * (1 - 2 * lax.rem(i, 2))
        return pltpu.make_async_remote_copy(
            src_ref=zrec,
            dst_ref=zbuf.at[iz],
            send_sem=z_ssem.at[step],
            recv_sem=z_rsem.at[step],
            device_id={"row": lax.rem(iz + step, nz)},
            device_id_type=MESH,
        )

    for i in range(nz - 1):
        along_z(i).start()
    for i in range(nz - 1):
        along_z(i).wait_recv()

    records = zbuf[...].reshape(nz, 128)
    energy, curve = pick(records, S0), pick(records, S1)
    first_step = energy / curve
    delta = first_step - pick(records, GUESS, axis=1)
    weight = by_lane(records.shape, [(Q0, one), (Q1, -2.0 * delta), (Q2, delta * delta)])
    energy_next = jnp.sum(weight * records, keepdims=True)
    weight = by_lane(records.shape, [(E0, one), (E1, -delta), (E2, delta * delta)])
    curve_next = jnp.sum(weight * records, keepdims=True)
    ratio = energy_next / energy
    second_step = energy_next / (curve_next - ratio * energy_next / first_step)
    both = first_step + second_step * (1.0 + ratio)
    back = first_step * second_step
    scal_ref[...] = by_lane(scal_ref.shape, [(0, first_step), (1, both), (2, back)])

    for turn in range(3):
        end_halo(turn)
    to_other(0, z_p, zother).wait_send()
    to_other(1, y_p, yother).wait_send()
    for step in range(1, np_):
        in_plane(step).wait_send()
    for i in range(nz - 1):
        along_z(i).wait_send()
    for copy in (save_z, save_w, save_y, save_u):
        copy.wait()


def local(nz, nx, nc, current, node_class, class_conductance, pad_mask, via_mask):
    rows, cols = via_mask.shape
    field = jax.ShapeDtypeStruct((rows, cols), jnp.float32)
    full = pltpu.VMEM((rows, cols), jnp.float32)
    whole = pltpu.VMEM((rows, cols), jnp.int32)
    padded = pltpu.VMEM((rows + 16, cols), jnp.float32)
    hbm = pl.BlockSpec(memory_space=pl.ANY)
    dma = pltpu.SemaphoreType.DMA
    scratch = [full, whole, whole, whole, padded, padded, padded, full, full, full, full, full]
    scratch += [
        pltpu.VMEM((3, 2, 1, cols), jnp.float32),
        pltpu.VMEM((3, 2, 8, 128), jnp.float32),
        pltpu.VMEM((3, 2, 1, cols), jnp.float32),
        pltpu.VMEM((3, 2, 8, 128), jnp.float32),
        pltpu.VMEM((1, 128), jnp.float32),
        pltpu.VMEM((nx * nc, 1, 128), jnp.float32),
        pltpu.VMEM((1, 128), jnp.float32),
        pltpu.VMEM((nz, 1, 128), jnp.float32),
        dma((4,)),
        dma((4,)),
        dma((3, 4)),
        dma((3, 4)),
        dma((2,)),
        dma((2,)),
        dma((nx * nc,)),
        dma((nx * nc,)),
        dma((nz,)),
        dma((nz,)),
        pltpu.SemaphoreType.REGULAR((4,)),
    ]
    z, w, y, u, scal = pl.pallas_call(
        functools.partial(kernel, nz, nx, nc),
        out_shape=[field] * 4 + [jax.ShapeDtypeStruct((8, 128), jnp.float32)],
        in_specs=[hbm, hbm, pl.BlockSpec(memory_space=pltpu.SMEM), hbm, hbm],
        out_specs=[hbm] * 4 + [pl.BlockSpec(memory_space=pltpu.VMEM)],
        scratch_shapes=scratch,
        compiler_params=pltpu.CompilerParams(
            collective_id=0, has_side_effects=True, vmem_limit_bytes=32 * 1024 * 1024
        ),
    )(current[0], node_class[0], class_conductance, pad_mask[0], via_mask)
    first_step, both, back = scal[0, 0], scal[0, 1], scal[0, 2]
    drop = both * z - back * y
    resid = current[0] - both * w + back * u
    worst = jnp.maximum(first_step * z, drop)
    return (drop[None], resid[None], worst[None])


def solution(mesh):
    grid = P("layer", ("scen", "row"), "col")
    in_specs = (grid, grid, P("layer", None), grid, P(("scen", "row"), "col"))
    sizes = (mesh.shape["row"], mesh.shape["col"], mesh.shape["layer"])
    return jax.shard_map(
        functools.partial(local, *sizes),
        mesh=mesh,
        in_specs=in_specs,
        out_specs=(grid, grid, grid),
        check_vma=False,
    )
```

time: 182 us -> 84.1 us (0.46)
  blocking collectives: 105 us -> 0 us
  Pallas kernels: 0 us -> 74.5 us
  starting transfers between devices: 37.6 us -> 0 us
  waiting for transfers between devices: 14.6 us -> 0 us
  other arithmetic: 14.5 us -> 3.14 us
  between operations: 7.14 us -> 0.65 us
  local copies, waits for them, and re-layouts: 2.5 us -> 5.46 us
    psum x3 -> x0, blocking collectives: 105 us -> none  [over_axes(): return functools.reduce(lax.psum, axes, value)]
    pallas_call x0 -> x1, Pallas kernels: none -> 74.5 us  [local(): pl.pallas_call(functools.partial(kernel, nz, nx, nc), out_shape=[field] *...]
    ppermute x14 -> x0, starting transfers between devices: 37.6 us -> none  [the longest x6 25.8 us: with_halo(): lax.ppermute(last, axis, up)]
    ppermute x14 -> x0, waiting for transfers between devices: 14.6 us -> none  [the longest x6 12.9 us: with_halo(): lax.ppermute(initial, axis, [(b, a) for a, b in up])]
    add x1 -> x0, other arithmetic: 6.58 us -> none  [lookup(): cond + jnp.where(node_class == klass, class_conductance[:, klass][:, None...]
    unnamed x4 -> x10, local copies, waits for them, and re-layouts: 0.01 us -> 4.81 us
    broadcast_in_dim x0 -> x1, other arithmetic: none -> 3.14 us  [local(): return (drop[None], resid[None], worst[None])]
    another operation x1 -> x0, other arithmetic: 2.57 us -> none  [local(): jnp.stack([jnp.sum(current * precond), jnp.sum(precond * image), jnp.sum(...]
  transfers between devices with their start and end apart: 14 -> 0, of which waited for: 6 -> 0; matrix products, arithmetic and copies ran while one was open for 0% -> 0% of each run, Pallas kernels for 0% -> 0%
where the time goes in v2:
time: 84.1 us; the launch traced here: 83.8 us
  Pallas kernels  74.5 us (89%)
  local copies, waits for them, and re-layouts  5.46 us (6%)
  other arithmetic  3.14 us (4%)
    pallas_call x1, Pallas kernels, local(): pl.pallas_call(functools.partial(kernel, nz, nx, nc), out_shape=[field] *...  74.5 us
    unnamed x10, local copies, waits for them, and re-layouts  4.81 us
    broadcast_in_dim x1, other arithmetic, local(): return (drop[None], resid[None], worst[None])  3.14 us

profile of v2, /device:TPU:40, one launch (start us, length us, event | category | flops | bytes accessed | tf_op | source)
XLA Modules:
  0.0 83.8 jit_solution(6624539617672388639)
XLA Ops:
  0.6 0.0 copy-start.4
  0.6 0.6 copy-done.4
  1.3 0.0 copy-start
  1.3 1.0 %copy-done = f32[1,128,1024]{2,1,0:T(8,128)S(1)} copy-done((f32[1,128,1024]{2,1,0:T(8,128)S(1)}, f32[1,128,1024]{2,1,0:T(8,128)}, u32[]{:S(2)}) %copy-start) | copy-done | bytes 524312
  2.3 0.0 copy-start.1
  2.3 1.0 %copy-done.1 = s32[1,128,1024]{2,1,0:T(8,128)S(1)} copy-done((s32[1,128,1024]{2,1,0:T(8,128)S(1)}, s32[1,128,1024]{2,1,0:T(8,128)}, u32[]{:S(2)}) %copy-start.1) | copy-done | bytes 524312
  3.4 0.0 copy-start.2
  3.4 1.0 %copy-done.2 = s32[1,128,1024]{2,1,0:T(8,128)S(1)} copy-done((s32[1,128,1024]{2,1,0:T(8,128)S(1)}, s32[1,128,1024]{2,1,0:T(8,128)}, u32[]{:S(2)}) %copy-start.2) | copy-done | bytes 524312
  4.4 0.0 copy-start.3
  4.4 1.0 %copy-done.3 = s32[128,1024]{1,0:T(8,128)S(1)} copy-done((s32[128,1024]{1,0:T(8,128)S(1)}, s32[128,1024]{1,0:T(8,128)}, u32[]{:S(2)}) %copy-start.3) | copy-done | bytes 524312
  5.5 74.5 %shard_map.76 = (f32[128,1024]{1,0:T(8,128)S(1)}, f32[128,1024]{1,0:T(8,128)S(1)}, f32[128,1024]{1,0:T(8,128)S(1)}, f32[128,1024]{1,0:T(8,128)S(1)}, f32[8,128]{1,0:T(8,128)S(1)}) custom-call(f32[128,1024]{1,0:T(8,128)S(1)} %bitcast.13, s32[128,1024]{1,0:T(8,128)S(1)} %bitcast.14, f32[1,8]{1,0:T(1,128)S(1)} %copy-done.4, s32[128,1024]{1,0:T(8,128)S(1)} %bitcast.15, ...), custom_call_target="tpu_custom_call" | custom-call | tf_op jit(solution)/shard_map/pallas_call | solution.py:453
  80.0 0.7 fusion.1
  80.6 3.1 %maximum_bitcast_fusion = (f32[1,128,1024]{2,1,0:T(8,128)}, f32[1,128,1024]{2,1,0:T(8,128)}, f32[1,128,1024]{2,1,0:T(8,128)}) fusion(f32[128,1024]{1,0:T(8,128)S(1)} %get-tuple-element.9, f32[128,1024]{1,0:T(8,128)S(1)} %get-tuple-element.10, f32[]{:T(128)} %bitcast.7, f32[]{:T(128)} %bitcast.4, f32[]{:T(128)} %bitcast.3, ...), kind=kLoop, calls=%fused_computation | loop fusion | flops 1179648 | bytes 4194316 | tf_op jit(solution)/shard_map/broadcast_in_dim | solution.py:467
Async XLA Ops:
  0.6 0.7 copy-start.4
  1.3 1.0 %copy-start = (f32[1,128,1024]{2,1,0:T(8,128)S(1)}, f32[1,128,1024]{2,1,0:T(8,128)}, u32[]{:S(2)}) copy-start(f32[1,128,1024]{2,1,0:T(8,128)} %param.5) | copy-start | bytes 1572868
  2.3 1.0 %copy-start.1 = (s32[1,128,1024]{2,1,0:T(8,128)S(1)}, s32[1,128,1024]{2,1,0:T(8,128)}, u32[]{:S(2)}) copy-start(s32[1,128,1024]{2,1,0:T(8,128)} %param.6) | copy-start | bytes 1572868
  3.4 1.0 %copy-start.2 = (s32[1,128,1024]{2,1,0:T(8,128)S(1)}, s32[1,128,1024]{2,1,0:T(8,128)}, u32[]{:S(2)}) copy-start(s32[1,128,1024]{2,1,0:T(8,128)} %param.8) | copy-start | bytes 1572868
  4.4 1.0 %copy-start.3 = (s32[128,1024]{1,0:T(8,128)S(1)}, s32[128,1024]{1,0:T(8,128)}, u32[]{:S(2)}) copy-start(s32[128,1024]{1,0:T(8,128)} %via_hbm.1) | copy-start | bytes 1572868

commit v3 on v2

--- a/solution.py
+++ b/solution.py
@@ -53,21 +53,19 @@
     cc_ref,
     pad_hbm,
     via_hbm,
-    z_hbm,
-    w_hbm,
-    y_hbm,
-    u_hbm,
+    cur,
+    z_p,
+    w,
+    y_p,
+    u,
     scal_ref,
-    cur,
     cls,
     pad,
     via,
     cond_p,
-    z_p,
-    y_p,
+    edges,
+    coupling,
     inv,
-    w,
-    u,
     zother,
     yother,
     srow,
@@ -79,7 +77,6 @@
     zrec,
     zbuf,
     in_sem,
-    out_sem,
     halo_ssem,
     halo_rsem,
     other_ssem,
@@ -92,6 +89,7 @@
 ):
     iz, ix, ic = lax.axis_index("row"), lax.axis_index("col"), lax.axis_index("layer")
     rows, cols = cur.shape
+    unroll = 2
     chunks = rows // 8
     np_ = nx * nc
     me = ix * nc + ic
@@ -216,7 +214,7 @@
             ],
             axis=1,
         )
-        return (up + down) + (west + east)
+        return up, down, west, east
 
     loads[0].wait()
 
@@ -229,7 +227,7 @@
         cond_p[at(k, 8), :] = level[0]
         return packed(k, level[0], *carry)
 
-    left, right = lax.fori_loop(0, chunks, look_up, (zero, zero))
+    left, right = lax.fori_loop(0, chunks, look_up, (zero, zero), unroll=unroll)
     send_halo(0, cond_p, left, right)
     greeted(0)
     greet(1)
@@ -237,10 +235,6 @@
         copy.wait()
     take_halo(0, cond_p)
 
-    lane = lanes_of(tile)
-    one = jnp.float32(1.0)
-    beside_x = 4.0 - jnp.where((lane == 0) & (ix == 0), one, 0.0)
-    beside_x = beside_x - jnp.where((lane == cols - 1) & (ix == nx - 1), one, 0.0)
     cond_left, cond_right = rcol[0, 0], rcol[0, 1]
 
     def precondition(k, carry):
@@ -249,13 +243,14 @@
         near = around(
             k, cond_p[at(k), :], here, cond_p[at(k, 16), :], cond_left, cond_right
         )
-        row = sub + 8 * k
-        beside = beside_x - jnp.where((row == 0) & (iz == 0), one, 0.0)
-        beside = beside - jnp.where((row == rows - 1) & (iz == nz - 1), one, 0.0)
-        diagonal = 0.5 * (beside * here + near)
-        diagonal = diagonal + via_conductance * via[at(k), :].astype(jnp.float32)
+        near = [jnp.where(other > 0.0, 0.5 * (here + other), 0.0) for other in near]
+        for i in range(4):
+            edges[i, at(k), :] = near[i]
+        across = via_conductance * via[at(k), :].astype(jnp.float32)
+        coupling[at(k), :] = across
+        diagonal = (near[0] + near[1]) + (near[2] + near[3])
         diagonal = diagonal + (
-            pad_conductance * pad[at(k), :].astype(jnp.float32) + leakage
+            across + pad_conductance * pad[at(k), :].astype(jnp.float32) + leakage
         )
         inverse = 1.0 / diagonal
         resid = cur[at(k), :]
@@ -265,24 +260,20 @@
         left, right = packed(k, value, left, right)
         return left, right, energy + fold(resid * value)
 
-    left, right, energy = lax.fori_loop(0, chunks, precondition, (zero, zero, zero))
+    left, right, energy = lax.fori_loop(0, chunks, precondition, (zero, zero, zero), unroll=unroll)
     to_other(0, z_p, zother).start()
     send_halo(1, z_p, left, right)
     greeted(1)
     greet(2)
-    save_z = pltpu.make_async_copy(z_p.at[pl.ds(8, rows)], z_hbm, out_sem.at[0])
-    save_z.start()
     take_halo(1, z_p)
     to_other(0, z_p, zother).wait_recv()
 
     def image(k, field, lead, left, right, other):
-        conds = [cond_p[at(k, 8 * i), :] for i in range(3)]
         values = [field[at(k, 8 * i), :] for i in range(3)]
-        flux = [a * b for a, b in zip(conds, values)]
-        plain = around(k, *values, left, right)
-        scaled = around(k, *flux, cond_left * left, cond_right * right)
-        across = via_conductance * via[at(k), :].astype(jnp.float32) * other[at(k), :]
-        return lead - 0.5 * (conds[1] * plain + scaled) - across, values[1]
+        near = around(k, *values, left, right)
+        terms = [edges[i, at(k), :] * near[i] for i in range(4)]
+        beside = (terms[0] + terms[1]) + (terms[2] + terms[3])
+        return lead - beside - coupling[at(k), :] * other[at(k), :], values[1]
 
     z_left, z_right = rcol[1, 0], rcol[1, 1]
 
@@ -295,15 +286,11 @@
         left, right = packed(k, nxt, left, right)
         return left, right, curve + fold(value * out)
 
-    left, right, curve = lax.fori_loop(0, chunks, first_image, (zero, zero, zero))
+    left, right, curve = lax.fori_loop(0, chunks, first_image, (zero, zero, zero), unroll=unroll)
     to_other(1, y_p, yother).start()
     send_halo(2, y_p, left, right)
     greeted(2)
     greet(3)
-    save_w = pltpu.make_async_copy(w, w_hbm, out_sem.at[1])
-    save_w.start()
-    save_y = pltpu.make_async_copy(y_p.at[pl.ds(8, rows)], y_hbm, out_sem.at[2])
-    save_y.start()
     energy = jnp.sum(energy, keepdims=True)
     curve = jnp.sum(curve, keepdims=True)
     guess = energy / curve
@@ -329,9 +316,7 @@
         )
         return tuple(a + fold(b) for a, b in zip(sums, terms))
 
-    sums = lax.fori_loop(0, chunks, second_image, (zero,) * 6)
-    save_u = pltpu.make_async_copy(u, u_hbm, out_sem.at[3])
-    save_u.start()
+    sums = lax.fori_loop(0, chunks, second_image, (zero,) * 6, unroll=unroll)
 
     line = (1, 128)
     entries = [(S0, energy), (S1, curve), (GUESS, guess)]
@@ -378,8 +363,7 @@
     greeted(3)
 
     def along_z(i):
-        away = (i + 1) // 2
-        step = nz // 2 + away * (1 - 2 * lax.rem(i, 2))
+        step = i // 2 + 1 if i % 2 == 0 else nz - 1 - i // 2
         return pltpu.make_async_remote_copy(
             src_ref=zrec,
             dst_ref=zbuf.at[iz],
@@ -398,15 +382,16 @@
     energy, curve = pick(records, S0), pick(records, S1)
     first_step = energy / curve
     delta = first_step - pick(records, GUESS, axis=1)
-    weight = by_lane(records.shape, [(Q0, one), (Q1, -2.0 * delta), (Q2, delta * delta)])
+    weight = by_lane(records.shape, [(Q0, 1.0), (Q1, -2.0 * delta), (Q2, delta * delta)])
     energy_next = jnp.sum(weight * records, keepdims=True)
-    weight = by_lane(records.shape, [(E0, one), (E1, -delta), (E2, delta * delta)])
+    weight = by_lane(records.shape, [(E0, 1.0), (E1, -delta), (E2, delta * delta)])
     curve_next = jnp.sum(weight * records, keepdims=True)
     ratio = energy_next / energy
     second_step = energy_next / (curve_next - ratio * energy_next / first_step)
     both = first_step + second_step * (1.0 + ratio)
     back = first_step * second_step
-    scal_ref[...] = by_lane(scal_ref.shape, [(0, first_step), (1, both), (2, back)])
+    for i, value in enumerate((first_step, both, back)):
+        scal_ref[i] = jnp.broadcast_to(value, block)
 
     for turn in range(3):
         end_halo(turn)
@@ -416,19 +401,46 @@
         in_plane(step).wait_send()
     for i in range(nz - 1):
         along_z(i).wait_send()
-    for copy in (save_z, save_w, save_y, save_u):
+
+
+def finish(cur, z_p, w, y_p, u, scal, drop_hbm, resid_hbm, worst_hbm, drop, resid, worst, sem):
+    rows, cols = cur.shape
+    pieces = 4
+    size = rows // pieces
+    wide = [jnp.concatenate([scal[i]] * (cols // 128), axis=1) for i in range(3)]
+    copies = []
+    for piece in range(pieces):
+        for k in range(size // 8):
+            at = pl.ds(piece * size + 8 * k, 8)
+            below = pl.ds(piece * size + 8 * k + 8, 8)
+            z = z_p[below, :]
+            new = wide[1] * z - wide[2] * y_p[below, :]
+            drop[at, :] = new
+            resid[at, :] = cur[at, :] - wide[1] * w[at, :] + wide[2] * u[at, :]
+            worst[at, :] = jnp.maximum(wide[0] * z, new)
+        part = pl.ds(piece * size, size)
+        for i, (src, dst) in enumerate(
+            ((drop, drop_hbm), (resid, resid_hbm), (worst, worst_hbm))
+        ):
+            copy = pltpu.make_async_copy(src.at[part], dst.at[part], sem.at[i, piece])
+            copy.start()
+            copies.append(copy)
+    for copy in copies:
         copy.wait()
 
 
 def local(nz, nx, nc, current, node_class, class_conductance, pad_mask, via_mask):
     rows, cols = via_mask.shape
     field = jax.ShapeDtypeStruct((rows, cols), jnp.float32)
+    tall = jax.ShapeDtypeStruct((rows + 16, cols), jnp.float32)
     full = pltpu.VMEM((rows, cols), jnp.float32)
     whole = pltpu.VMEM((rows, cols), jnp.int32)
     padded = pltpu.VMEM((rows + 16, cols), jnp.float32)
-    hbm = pl.BlockSpec(memory_space=pl.ANY)
+    hbm = pl.BlockSpec(memory_space=pltpu.HBM)
+    vmem = pl.BlockSpec(memory_space=pltpu.VMEM)
     dma = pltpu.SemaphoreType.DMA
-    scratch = [full, whole, whole, whole, padded, padded, padded, full, full, full, full, full]
+    scratch = [whole, whole, whole, padded, pltpu.VMEM((4, rows, cols), jnp.float32)]
+    scratch += [full] * 4
     scratch += [
         pltpu.VMEM((3, 2, 1, cols), jnp.float32),
         pltpu.VMEM((3, 2, 8, 128), jnp.float32),
@@ -438,7 +450,6 @@
         pltpu.VMEM((nx * nc, 1, 128), jnp.float32),
         pltpu.VMEM((1, 128), jnp.float32),
         pltpu.VMEM((nz, 1, 128), jnp.float32),
-        dma((4,)),
         dma((4,)),
         dma((3, 4)),
         dma((3, 4)),
@@ -450,21 +461,29 @@
         dma((nz,)),
         pltpu.SemaphoreType.REGULAR((4,)),
     ]
-    z, w, y, u, scal = pl.pallas_call(
+    limit = 32 * 1024 * 1024
+    scalars = jax.ShapeDtypeStruct((3, 8, 128), jnp.float32)
+    args = (current[0], node_class[0], class_conductance, pad_mask[0], via_mask)
+    stay = [pltpu.with_memory_space_constraint(arg, pltpu.HBM) for arg in args]
+    solved = pl.pallas_call(
         functools.partial(kernel, nz, nx, nc),
-        out_shape=[field] * 4 + [jax.ShapeDtypeStruct((8, 128), jnp.float32)],
+        out_shape=[field, tall, field, tall, field, scalars],
         in_specs=[hbm, hbm, pl.BlockSpec(memory_space=pltpu.SMEM), hbm, hbm],
-        out_specs=[hbm] * 4 + [pl.BlockSpec(memory_space=pltpu.VMEM)],
+        out_specs=[vmem] * 6,
         scratch_shapes=scratch,
         compiler_params=pltpu.CompilerParams(
-            collective_id=0, has_side_effects=True, vmem_limit_bytes=32 * 1024 * 1024
+            collective_id=0, has_side_effects=True, vmem_limit_bytes=limit
         ),
-    )(current[0], node_class[0], class_conductance, pad_mask[0], via_mask)
-    first_step, both, back = scal[0, 0], scal[0, 1], scal[0, 2]
-    drop = both * z - back * y
-    resid = current[0] - both * w + back * u
-    worst = jnp.maximum(first_step * z, drop)
-    return (drop[None], resid[None], worst[None])
+    )(*stay)
+    outs = pl.pallas_call(
+        finish,
+        out_shape=[field] * 3,
+        in_specs=[vmem] * 6,
+        out_specs=[hbm] * 3,
+        scratch_shapes=[full] * 3 + [dma((3, 4))],
+        compiler_params=pltpu.CompilerParams(vmem_limit_bytes=limit),
+    )(*solved)
+    return tuple(out[None] for out in outs)
 
 
 def solution(mesh):

time: 84.1 us -> 74.2 us (0.88)
  local copies, waits for them, and re-layouts: 5.46 us -> 0 us
  other arithmetic: 3.14 us -> 0 us
  Pallas kernels: 74.5 us -> 73.4 us
    unnamed x10 -> x0, local copies, waits for them, and re-layouts: 4.81 us -> none
    broadcast_in_dim x1 -> x0, other arithmetic: 3.14 us -> none  [local(): return (drop[None], resid[None], worst[None])]
    pallas_call x1 -> x2, Pallas kernels: 74.5 us -> 73.4 us  [the longest x1 72.2 us: local(): pl.pallas_call(functools.partial(kernel, nz, nx, nc), out_shape=[field, t...]
where the time goes in v3:
time: 74.2 us; the launch traced here: 74.1 us
  Pallas kernels  73.4 us (99%)
    pallas_call x1, Pallas kernels, local(): pl.pallas_call(functools.partial(kernel, nz, nx, nc), out_shape=[field, t...  72.2 us

profile of v3, /device:TPU:40, one launch (start us, length us, event | category | flops | bytes accessed | tf_op | source)
XLA Modules:
  0.0 74.1 jit_solution(14566166454961249014)
XLA Ops:
  0.6 72.2 %shard_map.76 = (f32[128,1024]{1,0:T(8,128)S(1)}, f32[144,1024]{1,0:T(8,128)S(1)}, f32[128,1024]{1,0:T(8,128)S(1)}, f32[144,1024]{1,0:T(8,128)S(1)}, f32[128,1024]{1,0:T(8,128)S(1)}, /*index=5*/f32[3,8,128]{2,1,0:T(8,128)S(1)}) custom-call(f32[128,1024]{1,0:T(8,128)} %bitcast.6, s32[128,1024]{1,0:T(8,128)} %bitcast.7, f32[1,8]{1,0:T(1,128)} %cc_ref.1, ...), custom_call_target="tpu_custom_call" | custom-call | tf_op jit(solution)/shard_map/pallas_call | solution.py:468
  72.8 1.3 %shard_map.77 = (f32[128,1024]{1,0:T(8,128)}, f32[128,1024]{1,0:T(8,128)}, f32[128,1024]{1,0:T(8,128)}) custom-call(f32[128,1024]{1,0:T(8,128)S(1)} %get-tuple-element.12.cur, f32[144,1024]{1,0:T(8,128)S(1)} %get-tuple-element.13.z_p, f32[128,1024]{1,0:T(8,128)S(1)} %get-tuple-element.14.w, f32[144,1024]{1,0:T(8,128)S(1)} %get-tuple-element.15.y_p, ...), custom_call_target="tpu_custom_call" | custom-call | tf_op jit(solution)/shard_map/pallas_call | solution.py:478

commit v4 on v3

--- a/solution.py
+++ b/solution.py
@@ -12,6 +12,8 @@
 via_conductance = 2.0
 pad_conductance = 4.0
 leakage = 0.05
+
+REACH = 2
 
 S0, S1, Q0, Q1, Q2, E0, E1, E2, GUESS = range(9)
 
@@ -65,15 +67,22 @@
     cond_p,
     edges,
     coupling,
+    base,
     inv,
     zother,
     yother,
-    srow,
-    scol,
-    rrow,
-    rcol,
+    raw_row,
+    raw_col,
+    raw_corner,
+    got_row,
+    got_col,
+    got_corner,
+    y_row,
+    y_col,
+    goty_row,
+    goty_col,
     srec,
-    plane,
+    near,
     zrec,
     zbuf,
     in_sem,
@@ -81,8 +90,8 @@
     halo_rsem,
     other_ssem,
     other_rsem,
-    plane_ssem,
-    plane_rsem,
+    near_ssem,
+    near_rsem,
     z_ssem,
     z_rsem,
     ready,
@@ -91,7 +100,7 @@
     rows, cols = cur.shape
     unroll = 2
     chunks = rows // 8
-    np_ = nx * nc
+    reach = REACH
     me = ix * nc + ic
 
     loads = [
@@ -103,21 +112,28 @@
     for copy in loads:
         copy.start()
 
-    rrow[...] = jnp.zeros(rrow.shape, jnp.float32)
-    rcol[...] = jnp.zeros(rcol.shape, jnp.float32)
-
+    for buffer in (got_row, got_col, got_corner, goty_row, goty_col, zbuf):
+        buffer[...] = jnp.zeros(buffer.shape, jnp.float32)
+
+    def device(dz, dx, dc=0):
+        where = {}
+        for name, index, size, step in (
+            ("row", iz, nz, dz),
+            ("col", ix, nx, dx),
+            ("layer", ic, nc, dc),
+        ):
+            if step % size:
+                where[name] = lax.rem(index + step % size, size)
+        return where
+
+    plane = [(dx, dc) for dx in range(nx) for dc in range(nc)]
+    greets = [(0, dx, dc) for dx, dc in plane[1:]]
+    greets += [(dz, dx, 0) for dz in (-1, 1) for dx in (0, -1, 1)]
     barrier = pltpu.get_barrier_semaphore()
-    zup, zdown = lax.rem(iz + nz - 1, nz), lax.rem(iz + 1, nz)
-    for near in (zup, zdown):
-        pl.semaphore_signal(barrier, inc=1, device_id={"row": near}, device_id_type=MESH)
-
-    def plane_peer(step):
-        other = lax.rem(me + step, np_)
-        return {"col": other // nc, "layer": lax.rem(other, nc)}
-
-    for step in range(1, np_):
-        pl.semaphore_signal(barrier, inc=1, device_id=plane_peer(step), device_id_type=MESH)
-    pl.semaphore_wait(barrier, np_ + 1)
+    for steps in greets:
+        pl.semaphore_signal(
+            barrier, inc=1, device_id=device(*steps), device_id_type=MESH
+        )
 
     levels = (nz // 2).bit_length() - 1
 
@@ -134,43 +150,57 @@
         if level < levels:
             pl.semaphore_wait(ready.at[level], 2)
 
-    greet(0)
-
-    sides = (
-        (srow, rrow, 0, 1, iz > 0, iz < nz - 1, {"row": iz - 1}),
-        (srow, rrow, 1, 0, iz < nz - 1, iz > 0, {"row": iz + 1}),
-        (scol, rcol, 0, 1, ix > 0, ix < nx - 1, {"col": ix - 1}),
-        (scol, rcol, 1, 0, ix < nx - 1, ix > 0, {"col": ix + 1}),
-    )
-
-    def halo(turn, i):
-        src, dst, mine, theirs, _, _, target = sides[i]
+    inside = {
+        ("row", -1): iz > 0,
+        ("row", 1): iz < nz - 1,
+        ("col", -1): ix > 0,
+        ("col", 1): ix < nx - 1,
+    }
+
+    def exists(dz, dx):
+        flags = [inside["row", dz]] if dz else []
+        flags += [inside["col", dx]] if dx else []
+        return functools.reduce(jnp.logical_and, flags)
+
+    slot = {-1: 0, 1: 1}
+    raw = [(dz, 0, raw_row.at[slot[dz]], got_row, slot[-dz]) for dz in (-1, 1)]
+    raw += [(0, dx, raw_col.at[slot[dx]], got_col, slot[-dx]) for dx in (-1, 1)]
+    raw += [
+        (
+            dz,
+            dx,
+            raw_corner.at[2 * slot[dz] + slot[dx]],
+            got_corner,
+            2 * slot[-dz] + slot[-dx],
+        )
+        for dz in (-1, 1)
+        for dx in (-1, 1)
+    ]
+    image_halo = [(dz, 0, y_row.at[slot[dz]], goty_row, slot[-dz]) for dz in (-1, 1)]
+    image_halo += [(0, dx, y_col.at[slot[dx]], goty_col, slot[-dx]) for dx in (-1, 1)]
+
+    def halo(turn, table, i):
+        dz, dx, src, dst, there = table[i]
         return pltpu.make_async_remote_copy(
-            src_ref=src.at[turn, mine],
-            dst_ref=dst.at[turn, theirs],
+            src_ref=src,
+            dst_ref=dst.at[there],
             send_sem=halo_ssem.at[turn, i],
             recv_sem=halo_rsem.at[turn, i],
-            device_id=target,
+            device_id=device(dz, dx),
             device_id_type=MESH,
         )
 
-    def send_halo(turn, field, left, right):
-        srow[turn, 0] = field[8:9, :]
-        srow[turn, 1] = field[rows + 7 : rows + 8, :]
-        scol[turn, 0] = left
-        scol[turn, 1] = right
-        for i in range(4):
-            pl.when(sides[i][4])(halo(turn, i).start)
-
-    def take_halo(turn, field):
-        for i in range(4):
-            pl.when(sides[i][5])(halo(turn, i).wait_recv)
-        field[0:8, :] = jnp.broadcast_to(rrow[turn, 0], (8, cols))
-        field[rows + 8 : rows + 16, :] = jnp.broadcast_to(rrow[turn, 1], (8, cols))
-
-    def end_halo(turn):
-        for i in range(4):
-            pl.when(sides[i][4])(halo(turn, i).wait_send)
+    def send_halo(turn, table):
+        for i, (dz, dx, *_) in enumerate(table):
+            pl.when(exists(dz, dx))(halo(turn, table, i).start)
+
+    def take_halo(turn, table):
+        for i, (dz, dx, *_) in enumerate(table):
+            pl.when(exists(-dz, -dx))(halo(turn, table, i).wait_recv)
+
+    def end_halo(turn, table):
+        for i, (dz, dx, *_) in enumerate(table):
+            pl.when(exists(dz, dx))(halo(turn, table, i).wait_send)
 
     def to_other(turn, src, dst):
         return pltpu.make_async_remote_copy(
@@ -216,7 +246,13 @@
         )
         return up, down, west, east
 
-    loads[0].wait()
+    for copy in loads:
+        copy.wait()
+    last = cols - 128
+
+    def place(k, value, lane, out):
+        moved = pltpu.roll(value, lax.rem(k + 128 - lane, 128), 1)
+        return jnp.where(narrow_lane == k, moved, out)
 
     def look_up(k, carry):
         klass = cls[at(k), :]
@@ -224,58 +260,123 @@
         for bit in range(3):
             high = (klass & (1 << bit)) != 0
             level = [jnp.where(high, b, a) for a, b in zip(level[::2], level[1::2])]
-        cond_p[at(k, 8), :] = level[0]
-        return packed(k, level[0], *carry)
-
-    left, right = lax.fori_loop(0, chunks, look_up, (zero, zero), unroll=unroll)
-    send_halo(0, cond_p, left, right)
+        cond = level[0]
+        cond_p[at(k, 8), :] = cond
+        across = via_conductance * via[at(k), :].astype(jnp.float32)
+        coupling[at(k), :] = across
+        rest = across + (pad_conductance * pad[at(k), :].astype(jnp.float32) + leakage)
+        base[at(k), :] = rest
+        load = cur[at(k), :]
+        borders = (
+            (cond[:, :128], 0),
+            (cond[:, :128], 1),
+            (rest[:, :128], 0),
+            (load[:, :128], 0),
+            (cond[:, last:], 127),
+            (cond[:, last:], 126),
+            (rest[:, last:], 127),
+            (load[:, last:], 127),
+        )
+        return tuple(place(k, *border, out) for border, out in zip(borders, carry))
+
+    packs = lax.fori_loop(0, chunks, look_up, (zero,) * 8, unroll=unroll)
+    for i in range(8):
+        raw_col[i // 4, i % 4] = packs[i]
+    for side, row in ((0, 0), (1, rows - 1)):
+        inward = 1 - 2 * side
+        raw_row[side, 0] = cond_p[8 + row : 9 + row, :]
+        raw_row[side, 1] = cond_p[8 + row + inward : 9 + row + inward, :]
+        raw_row[side, 2] = base[row : row + 1, :]
+        raw_row[side, 3] = cur[row : row + 1, :]
+        for end, col in ((0, 0), (1, cols - 1)):
+            corner = cond_p[8 + row : 9 + row, col : col + 1]
+            raw_corner[2 * side + end] = jnp.broadcast_to(corner, block)
+
+    pl.semaphore_wait(barrier, len(greets))
+    greet(0)
+    send_halo(0, raw)
     greeted(0)
     greet(1)
-    for copy in loads[1:]:
-        copy.wait()
-    take_halo(0, cond_p)
-
-    cond_left, cond_right = rcol[0, 0], rcol[0, 1]
-
-    def precondition(k, carry):
-        left, right, energy = carry
+    take_halo(0, raw)
+    for side, row in ((0, 0), (1, rows + 8)):
+        cond_p[row : row + 8, :] = jnp.broadcast_to(got_row[side, 0], tile)
+
+    cond_left, cond_right = got_col[0, 0], got_col[1, 0]
+
+    def edge(here, other):
+        return jnp.where(other > 0.0, 0.5 * (here + other), 0.0)
+
+    def precondition(k, energy):
         here = cond_p[at(k, 8), :]
-        near = around(
+        sides = around(
             k, cond_p[at(k), :], here, cond_p[at(k, 16), :], cond_left, cond_right
         )
-        near = [jnp.where(other > 0.0, 0.5 * (here + other), 0.0) for other in near]
+        sides = [edge(here, other) for other in sides]
         for i in range(4):
-            edges[i, at(k), :] = near[i]
-        across = via_conductance * via[at(k), :].astype(jnp.float32)
-        coupling[at(k), :] = across
-        diagonal = (near[0] + near[1]) + (near[2] + near[3])
-        diagonal = diagonal + (
-            across + pad_conductance * pad[at(k), :].astype(jnp.float32) + leakage
-        )
+            edges[i, at(k), :] = sides[i]
+        diagonal = ((sides[0] + sides[1]) + (sides[2] + sides[3])) + base[at(k), :]
         inverse = 1.0 / diagonal
         resid = cur[at(k), :]
         value = resid * inverse
         inv[at(k), :] = inverse
         z_p[at(k, 8), :] = value
-        left, right = packed(k, value, left, right)
-        return left, right, energy + fold(resid * value)
-
-    left, right, energy = lax.fori_loop(0, chunks, precondition, (zero, zero, zero), unroll=unroll)
+        return energy + fold(resid * value)
+
+    energy = lax.fori_loop(0, chunks, precondition, zero, unroll=unroll)
     to_other(0, z_p, zother).start()
-    send_halo(1, z_p, left, right)
     greeted(1)
     greet(2)
-    take_halo(1, z_p)
+
+    def beyond(here, others, rest, load):
+        sides = [edge(here, other) for other in others]
+        diagonal = ((sides[0] + sides[1]) + (sides[2] + sides[3])) + rest
+        return jnp.where(here > 0.0, load * (1.0 / diagonal), 0.0)
+
+    for side, row, inner in ((0, 0, 8), (1, rows + 8, rows + 7)):
+        here, outer, rest, load = [
+            jnp.broadcast_to(got_row[side, i], tile) for i in range(4)
+        ]
+        inner = jnp.broadcast_to(cond_p[inner : inner + 1, :], tile)
+        west = pltpu.roll(here, 1, 1)
+        west = jnp.concatenate(
+            [
+                jnp.where(narrow_lane == 0, got_corner[2 * side], west[:, :128]),
+                west[:, 128:],
+            ],
+            axis=1,
+        )
+        east = pltpu.roll(here, cols - 1, 1)
+        east = jnp.concatenate(
+            [
+                east[:, :last],
+                jnp.where(narrow_lane == 127, got_corner[2 * side + 1], east[:, last:]),
+            ],
+            axis=1,
+        )
+        z_p[row : row + 8, :] = beyond(here, (outer, inner, west, east), rest, load)
+
+    narrow_sub = rows_of(block)
+    z_ends = []
+    for side in range(2):
+        here, outer, rest, load = [got_col[side, i] for i in range(4)]
+        up = pltpu.roll(here, 1, 0)
+        up = jnp.where(narrow_sub == 0, pltpu.roll(up, 1, 1), up)
+        up = jnp.where((narrow_sub == 0) & (narrow_lane == 0), got_corner[side], up)
+        down = pltpu.roll(here, 7, 0)
+        down = jnp.where(narrow_sub == 7, pltpu.roll(down, 127, 1), down)
+        end = (narrow_sub == 7) & (narrow_lane == chunks - 1)
+        down = jnp.where(end, got_corner[2 + side], down)
+        inner = raw_col[side, 0]
+        z_ends.append(beyond(here, (up, down, outer, inner), rest, load))
+    z_left, z_right = z_ends
     to_other(0, z_p, zother).wait_recv()
 
     def image(k, field, lead, left, right, other):
         values = [field[at(k, 8 * i), :] for i in range(3)]
-        near = around(k, *values, left, right)
-        terms = [edges[i, at(k), :] * near[i] for i in range(4)]
+        sides = around(k, *values, left, right)
+        terms = [edges[i, at(k), :] * sides[i] for i in range(4)]
         beside = (terms[0] + terms[1]) + (terms[2] + terms[3])
         return lead - beside - coupling[at(k), :] * other[at(k), :], values[1]
-
-    z_left, z_right = rcol[1, 0], rcol[1, 1]
 
     def first_image(k, carry):
         left, right, curve = carry
@@ -288,16 +389,22 @@
 
     left, right, curve = lax.fori_loop(0, chunks, first_image, (zero, zero, zero), unroll=unroll)
     to_other(1, y_p, yother).start()
-    send_halo(2, y_p, left, right)
+    y_row[0] = y_p[8:9, :]
+    y_row[1] = y_p[rows + 7 : rows + 8, :]
+    y_col[0] = left
+    y_col[1] = right
+    send_halo(1, image_halo)
     greeted(2)
     greet(3)
     energy = jnp.sum(energy, keepdims=True)
     curve = jnp.sum(curve, keepdims=True)
     guess = energy / curve
-    take_halo(2, y_p)
+    take_halo(1, image_halo)
+    for side, row in ((0, 0), (1, rows + 8)):
+        y_p[row : row + 8, :] = jnp.broadcast_to(goty_row[side], tile)
     to_other(1, y_p, yother).wait_recv()
 
-    y_left, y_right = rcol[2, 0], rcol[2, 1]
+    y_left, y_right = goty_col[0], goty_col[1]
 
     def second_image(k, sums):
         along = w[at(k), :]
@@ -326,24 +433,28 @@
     ]
     record = by_lane(line, entries)
     srec[...] = record
-    plane[me] = record
-
-    def in_plane(step):
+    near[reach, me] = record
+
+    shifts = [0] + [dz for far in range(1, reach + 1) for dz in (far, -far)]
+    hops = [(dz, i) for dz in shifts for i in range(len(plane)) if dz or i]
+
+    def close(dz, i):
         return pltpu.make_async_remote_copy(
             src_ref=srec,
-            dst_ref=plane.at[me],
-            send_sem=plane_ssem.at[step],
-            recv_sem=plane_rsem.at[step],
-            device_id=plane_peer(step),
+            dst_ref=near.at[reach - dz, me],
+            send_sem=near_ssem.at[reach - dz, i],
+            recv_sem=near_rsem.at[reach - dz, i],
+            device_id=device(dz, *plane[i]),
             device_id_type=MESH,
         )
 
-    for step in range(1, np_):
-        in_plane(step).start()
-    for step in range(1, np_):
-        in_plane(step).wait_recv()
-
-    records = plane[...].reshape(np_, 128)
+    for hop in hops:
+        close(*hop).start()
+    for hop in hops:
+        if not hop[0]:
+            close(*hop).wait_recv()
+
+    records = near[reach].reshape(len(plane), 128)
     joint = pick(records, S0) / pick(records, S1)
     delta = joint - pick(records, GUESS, axis=1)
     first = by_lane(
@@ -359,26 +470,31 @@
     record = jnp.sum(records, axis=0, keepdims=True)
     record = jnp.where(lanes_of(line) == GUESS, joint, record)
     zrec[...] = record
-    zbuf[iz] = record
     greeted(3)
 
-    def along_z(i):
-        step = i // 2 + 1 if i % 2 == 0 else nz - 1 - i // 2
+    far = [i for pair in zip(range(1, nz), range(nz - 1, 0, -1)) for i in pair]
+    far = [i for i in dict.fromkeys(far) if reach < i < nz - reach]
+
+    def along_z(step):
         return pltpu.make_async_remote_copy(
             src_ref=zrec,
             dst_ref=zbuf.at[iz],
             send_sem=z_ssem.at[step],
             recv_sem=z_rsem.at[step],
-            device_id={"row": lax.rem(iz + step, nz)},
+            device_id=device(step, 0),
             device_id_type=MESH,
         )
 
-    for i in range(nz - 1):
-        along_z(i).start()
-    for i in range(nz - 1):
-        along_z(i).wait_recv()
-
-    records = zbuf[...].reshape(nz, 128)
+    for step in far:
+        along_z(step).start()
+    for step in far:
+        along_z(step).wait_recv()
+    for hop in hops:
+        if hop[0]:
+            close(*hop).wait_recv()
+
+    records = [near[i].reshape(len(plane), 128) for i in range(2 * reach + 1)]
+    records = jnp.concatenate(records + [zbuf[...].reshape(nz, 128)], axis=0)
     energy, curve = pick(records, S0), pick(records, S1)
     first_step = energy / curve
     delta = first_step - pick(records, GUESS, axis=1)
@@ -393,14 +509,14 @@
     for i, value in enumerate((first_step, both, back)):
         scal_ref[i] = jnp.broadcast_to(value, block)
 
-    for turn in range(3):
-        end_halo(turn)
+    end_halo(0, raw)
+    end_halo(1, image_halo)
     to_other(0, z_p, zother).wait_send()
     to_other(1, y_p, yother).wait_send()
-    for step in range(1, np_):
-        in_plane(step).wait_send()
-    for i in range(nz - 1):
-        along_z(i).wait_send()
+    for hop in hops:
+        close(*hop).wait_send()
+    for step in far:
+        along_z(step).wait_send()
 
 
 def finish(cur, z_p, w, y_p, u, scal, drop_hbm, resid_hbm, worst_hbm, drop, resid, worst, sem):
@@ -440,23 +556,29 @@
     vmem = pl.BlockSpec(memory_space=pltpu.VMEM)
     dma = pltpu.SemaphoreType.DMA
     scratch = [whole, whole, whole, padded, pltpu.VMEM((4, rows, cols), jnp.float32)]
-    scratch += [full] * 4
+    scratch += [full] * 5
+    near = (2 * REACH + 1, nx * nc)
     scratch += [
-        pltpu.VMEM((3, 2, 1, cols), jnp.float32),
-        pltpu.VMEM((3, 2, 8, 128), jnp.float32),
-        pltpu.VMEM((3, 2, 1, cols), jnp.float32),
-        pltpu.VMEM((3, 2, 8, 128), jnp.float32),
+        pltpu.VMEM((2, 4, 1, cols), jnp.float32),
+        pltpu.VMEM((2, 4, 8, 128), jnp.float32),
+        pltpu.VMEM((4, 8, 128), jnp.float32),
+    ] * 2
+    scratch += [
+        pltpu.VMEM((2, 1, cols), jnp.float32),
+        pltpu.VMEM((2, 8, 128), jnp.float32),
+    ] * 2
+    scratch += [
         pltpu.VMEM((1, 128), jnp.float32),
-        pltpu.VMEM((nx * nc, 1, 128), jnp.float32),
+        pltpu.VMEM((*near, 1, 128), jnp.float32),
         pltpu.VMEM((1, 128), jnp.float32),
         pltpu.VMEM((nz, 1, 128), jnp.float32),
         dma((4,)),
-        dma((3, 4)),
-        dma((3, 4)),
+        dma((2, 8)),
+        dma((2, 8)),
         dma((2,)),
         dma((2,)),
-        dma((nx * nc,)),
-        dma((nx * nc,)),
+        dma(near),
+        dma(near),
         dma((nz,)),
         dma((nz,)),
         pltpu.SemaphoreType.REGULAR((4,)),

time: 74.2 us -> 74.8 us (level)
  no operation moved by 1% of the time
where the time goes in v4:
time: 74.8 us; the launch traced here: 74.6 us
  Pallas kernels  74 us (99%)
    pallas_call x1, Pallas kernels, local(): pl.pallas_call(functools.partial(kernel, nz, nx, nc), out_shape=[field, t...  72.7 us

profile of v4, /device:TPU:40, one launch (start us, length us, event | category | flops | bytes accessed | tf_op | source)
XLA Modules:
  0.0 74.6 jit_solution(7321512506017581726)
XLA Ops:
  0.6 72.7 %shard_map.76 = (f32[128,1024]{1,0:T(8,128)S(1)}, f32[144,1024]{1,0:T(8,128)S(1)}, f32[128,1024]{1,0:T(8,128)S(1)}, f32[144,1024]{1,0:T(8,128)S(1)}, f32[128,1024]{1,0:T(8,128)S(1)}, /*index=5*/f32[3,8,128]{2,1,0:T(8,128)S(1)}) custom-call(f32[128,1024]{1,0:T(8,128)} %bitcast.6, s32[128,1024]{1,0:T(8,128)} %bitcast.7, f32[1,8]{1,0:T(1,128)} %cc_ref.1, ...), custom_call_target="tpu_custom_call" | custom-call | tf_op jit(solution)/shard_map/pallas_call | solution.py:590
  73.3 1.3 %shard_map.77 = (f32[128,1024]{1,0:T(8,128)}, f32[128,1024]{1,0:T(8,128)}, f32[128,1024]{1,0:T(8,128)}) custom-call(f32[128,1024]{1,0:T(8,128)S(1)} %get-tuple-element.12.cur, f32[144,1024]{1,0:T(8,128)S(1)} %get-tuple-element.13.z_p, f32[128,1024]{1,0:T(8,128)S(1)} %get-tuple-element.14.w, f32[144,1024]{1,0:T(8,128)S(1)} %get-tuple-element.15.y_p, ...), custom_call_target="tpu_custom_call" | custom-call | tf_op jit(solution)/shard_map/pallas_call | solution.py:600

commit v5 on v4

--- a/solution.py
+++ b/solution.py
@@ -94,7 +94,9 @@
     near_rsem,
     z_ssem,
     z_rsem,
-    ready,
+    low,
+    zero_in,
+    high,
 ):
     iz, ix, ic = lax.axis_index("row"), lax.axis_index("col"), lax.axis_index("layer")
     rows, cols = cur.shape
@@ -127,28 +129,53 @@
         return where
 
     plane = [(dx, dc) for dx in range(nx) for dc in range(nc)]
-    greets = [(0, dx, dc) for dx, dc in plane[1:]]
-    greets += [(dz, dx, 0) for dz in (-1, 1) for dx in (0, -1, 1)]
+    greets = {0: [(0, dx, dc) for dx, dc in plane[1:]]}
+    greets |= {dz: [(dz, dx, 0) for dx in (0, -1, 1)] for dz in (-1, 1)}
+    beside = {0: True, -1: iz > 0, 1: iz < nz - 1}
     barrier = pltpu.get_barrier_semaphore()
-    for steps in greets:
+
+    def greet(dz):
+        for steps in greets[dz]:
+            pl.semaphore_signal(
+                barrier, inc=1, device_id=device(*steps), device_id_type=MESH
+            )
+
+    for dz in greets:
+        pl.when(beside[dz])(functools.partial(greet, dz))
+
+    early = nz - 5
+
+    def tell(semaphore, row):
         pl.semaphore_signal(
-            barrier, inc=1, device_id=device(*steps), device_id_type=MESH
-        )
-
-    levels = (nz // 2).bit_length() - 1
-
-    def greet(level):
-        if level >= levels:
-            return
-        far = 1 << level
-        for near in (lax.rem(iz + far, nz), lax.rem(iz + nz - far, nz)):
-            pl.semaphore_signal(
-                ready.at[level], inc=1, device_id={"row": near}, device_id_type=MESH
-            )
-
-    def greeted(level):
-        if level < levels:
-            pl.semaphore_wait(ready.at[level], 2)
+            semaphore, inc=1, device_id={"row": row}, device_id_type=MESH
+        )
+
+    def announce():
+        pl.when(iz >= 2)(lambda: pl.semaphore_wait(low, 1))
+        pl.when((iz >= 1) & (iz < nz - 1))(lambda: tell(low, iz + 1))
+
+        def one(row, carry):
+            tell(high.at[iz], row)
+            return carry
+
+        lax.fori_loop(1, iz, one, 0)
+
+    def learn(row):
+        pl.semaphore_wait(high.at[row], 1)
+        pl.when(iz == 1)(lambda: tell(high.at[row], 0))
+        pl.when(iz == 0)(lambda: tell(zero_in, row))
+
+    def meet(row):
+        known = (iz <= 1) & (row <= jnp.maximum(early, 1))
+        pl.when((row > iz) & jnp.logical_not(known))(lambda: learn(row))
+        pl.when((row == 0) & (iz >= 2))(lambda: pl.semaphore_wait(zero_in, 1))
+
+    def learn_early():
+        def one(row, carry):
+            learn(row)
+            return carry
+
+        lax.fori_loop(2, early + 1, one, 0)
 
     inside = {
         ("row", -1): iz > 0,
@@ -292,11 +319,11 @@
             corner = cond_p[8 + row : 9 + row, col : col + 1]
             raw_corner[2 * side + end] = jnp.broadcast_to(corner, block)
 
-    pl.semaphore_wait(barrier, len(greets))
-    greet(0)
+    neighbours = jnp.minimum(iz, 1) + jnp.minimum(nz - 1 - iz, 1)
+    pl.semaphore_wait(barrier, len(greets[0]) + len(greets[1]) * neighbours)
     send_halo(0, raw)
-    greeted(0)
-    greet(1)
+    announce()
+    pl.when(iz <= 1)(learn_early)
     take_halo(0, raw)
     for side, row in ((0, 0), (1, rows + 8)):
         cond_p[row : row + 8, :] = jnp.broadcast_to(got_row[side, 0], tile)
@@ -324,8 +351,6 @@
 
     energy = lax.fori_loop(0, chunks, precondition, zero, unroll=unroll)
     to_other(0, z_p, zother).start()
-    greeted(1)
-    greet(2)
 
     def beyond(here, others, rest, load):
         sides = [edge(here, other) for other in others]
@@ -394,8 +419,6 @@
     y_col[0] = left
     y_col[1] = right
     send_halo(1, image_halo)
-    greeted(2)
-    greet(3)
     energy = jnp.sum(energy, keepdims=True)
     curve = jnp.sum(curve, keepdims=True)
     guess = energy / curve
@@ -448,8 +471,12 @@
             device_id_type=MESH,
         )
 
-    for hop in hops:
-        close(*hop).start()
+    for dz in shifts:
+        if dz:
+            meet(lax.rem(iz + dz + nz, nz))
+        for hop in hops:
+            if hop[0] == dz:
+                close(*hop).start()
     for hop in hops:
         if not hop[0]:
             close(*hop).wait_recv()
@@ -470,25 +497,43 @@
     record = jnp.sum(records, axis=0, keepdims=True)
     record = jnp.where(lanes_of(line) == GUESS, joint, record)
     zrec[...] = record
-    greeted(3)
-
-    far = [i for pair in zip(range(1, nz), range(nz - 1, 0, -1)) for i in pair]
-    far = [i for i in dict.fromkeys(far) if reach < i < nz - reach]
-
-    def along_z(step):
+
+    def along_z(row):
         return pltpu.make_async_remote_copy(
             src_ref=zrec,
             dst_ref=zbuf.at[iz],
-            send_sem=z_ssem.at[step],
-            recv_sem=z_rsem.at[step],
-            device_id=device(step, 0),
+            send_sem=z_ssem.at[row],
+            recv_sem=z_rsem.at[iz],
+            device_id={"row": row},
             device_id_type=MESH,
         )
 
-    for step in far:
-        along_z(step).start()
-    for step in far:
-        along_z(step).wait_recv()
+    def from_z(row):
+        return pltpu.make_async_remote_copy(
+            src_ref=zrec,
+            dst_ref=zbuf.at[row],
+            send_sem=z_ssem.at[row],
+            recv_sem=z_rsem.at[row],
+            device_id={"row": row},
+            device_id_type=MESH,
+        )
+
+    def far_rows(first, stop, act):
+        def one(row, carry):
+            away = jnp.abs(row - iz)
+            pl.when((away > reach) & (away < nz - reach))(lambda: act(row))
+            return carry
+
+        lax.fori_loop(first, stop, one, 0)
+
+    def met_send(row):
+        meet(row)
+        along_z(row).start()
+
+    far_rows(1, iz, lambda row: along_z(row).start())
+    far_rows(0, jnp.minimum(iz, 1), met_send)
+    far_rows(iz + 1, nz, met_send)
+    far_rows(0, nz, lambda row: from_z(row).wait_recv())
     for hop in hops:
         if hop[0]:
             close(*hop).wait_recv()
@@ -515,8 +560,7 @@
     to_other(1, y_p, yother).wait_send()
     for hop in hops:
         close(*hop).wait_send()
-    for step in far:
-        along_z(step).wait_send()
+    far_rows(0, nz, lambda row: along_z(row).wait_send())
 
 
 def finish(cur, z_p, w, y_p, u, scal, drop_hbm, resid_hbm, worst_hbm, drop, resid, worst, sem):
@@ -581,7 +625,9 @@
         dma(near),
         dma((nz,)),
         dma((nz,)),
-        pltpu.SemaphoreType.REGULAR((4,)),
+        pltpu.SemaphoreType.REGULAR,
+        pltpu.SemaphoreType.REGULAR,
+        pltpu.SemaphoreType.REGULAR((nz,)),
     ]
     limit = 32 * 1024 * 1024
     scalars = jax.ShapeDtypeStruct((3, 8, 128), jnp.float32)

time: 74.8 us -> 104 us (1.39)
  the two profiles are of different devices: /device:TPU:40 before, /device:TPU:33 now
where the time goes in v5:
time: 104 us
  Pallas kernels  103 us (99%)
    pallas_call x1, Pallas kernels, local(): pl.pallas_call(functools.partial(kernel, nz, nx, nc), out_shape=[field, t...  102 us

profile of v5, /device:TPU:33, one launch (start us, length us, event | category | flops | bytes accessed | tf_op | source)
XLA Modules:
  0.0 104.1 jit_solution(4935237357399478796)
XLA Ops:
  0.6 102.2 %shard_map.76 = (f32[128,1024]{1,0:T(8,128)S(1)}, f32[144,1024]{1,0:T(8,128)S(1)}, f32[128,1024]{1,0:T(8,128)S(1)}, f32[144,1024]{1,0:T(8,128)S(1)}, f32[128,1024]{1,0:T(8,128)S(1)}, /*index=5*/f32[3,8,128]{2,1,0:T(8,128)S(1)}) custom-call(f32[128,1024]{1,0:T(8,128)} %bitcast.6, s32[128,1024]{1,0:T(8,128)} %bitcast.7, f32[1,8]{1,0:T(1,128)} %cc_ref.1, ...), custom_call_target="tpu_custom_call" | custom-call | tf_op jit(solution)/shard_map/pallas_call | solution.py:636
  102.8 1.3 %shard_map.77 = (f32[128,1024]{1,0:T(8,128)}, f32[128,1024]{1,0:T(8,128)}, f32[128,1024]{1,0:T(8,128)}) custom-call(f32[128,1024]{1,0:T(8,128)S(1)} %get-tuple-element.12.cur, f32[144,1024]{1,0:T(8,128)S(1)} %get-tuple-element.13.z_p, f32[128,1024]{1,0:T(8,128)S(1)} %get-tuple-element.14.w, f32[144,1024]{1,0:T(8,128)S(1)} %get-tuple-element.15.y_p, ...), custom_call_target="tpu_custom_call" | custom-call | tf_op jit(solution)/shard_map/pallas_call | solution.py:646

commit v6 on v5

--- a/solution.py
+++ b/solution.py
@@ -13,7 +13,8 @@
 pad_conductance = 4.0
 leakage = 0.05
 
-REACH = 2
+REACH = 3
+PIECES = 4
 
 S0, S1, Q0, Q1, Q2, E0, E1, E2, GUESS = range(9)
 
@@ -52,7 +53,7 @@
     nc,
     cur_hbm,
     cls_hbm,
-    cc_ref,
+    cc_hbm,
     pad_hbm,
     via_hbm,
     cur,
@@ -61,6 +62,7 @@
     y_p,
     u,
     scal_ref,
+    cc_ref,
     cls,
     pad,
     via,
@@ -94,6 +96,8 @@
     near_rsem,
     z_ssem,
     z_rsem,
+    mid_rsem,
+    pass_sem,
     low,
     zero_in,
     high,
@@ -108,13 +112,13 @@
     loads = [
         pltpu.make_async_copy(src, dst, in_sem.at[i])
         for i, (src, dst) in enumerate(
-            ((cls_hbm, cls), (cur_hbm, cur), (pad_hbm, pad), (via_hbm, via))
+            ((cc_hbm, cc_ref), (cls_hbm, cls), (cur_hbm, cur), (pad_hbm, pad), (via_hbm, via))
         )
     ]
     for copy in loads:
         copy.start()
 
-    for buffer in (got_row, got_col, got_corner, goty_row, goty_col, zbuf):
+    for buffer in (got_row, got_col, got_corner, goty_row, goty_col, near, zbuf):
         buffer[...] = jnp.zeros(buffer.shape, jnp.float32)
 
     def device(dz, dx, dc=0):
@@ -129,21 +133,22 @@
         return where
 
     plane = [(dx, dc) for dx in range(nx) for dc in range(nc)]
-    greets = {0: [(0, dx, dc) for dx, dc in plane[1:]]}
-    greets |= {dz: [(dz, dx, 0) for dx in (0, -1, 1)] for dz in (-1, 1)}
-    beside = {0: True, -1: iz > 0, 1: iz < nz - 1}
+    greets = [(0, dx, dc) for dx, dc in plane[1:]]
+    greets += [(dz, dx, 0) for dz in (-1, 1) for dx in (0, -1, 1)]
     barrier = pltpu.get_barrier_semaphore()
-
-    def greet(dz):
-        for steps in greets[dz]:
-            pl.semaphore_signal(
-                barrier, inc=1, device_id=device(*steps), device_id_type=MESH
-            )
-
-    for dz in greets:
-        pl.when(beside[dz])(functools.partial(greet, dz))
-
-    early = nz - 5
+    for steps in greets:
+        pl.semaphore_signal(
+            barrier, inc=1, device_id=device(*steps), device_id_type=MESH
+        )
+
+    early = max(nz - 5, 2)
+
+    mid_first, mid_stop = max(nz // 4, 2), min(3 * nz // 4, nz - 1 - reach) + 1
+    mids = mid_stop - mid_first
+
+    def middle(row):
+        return (row >= mid_first) & (row < mid_stop)
+
 
     def tell(semaphore, row):
         pl.semaphore_signal(
@@ -151,8 +156,8 @@
         )
 
     def announce():
-        pl.when(iz >= 2)(lambda: pl.semaphore_wait(low, 1))
-        pl.when((iz >= 1) & (iz < nz - 1))(lambda: tell(low, iz + 1))
+        pl.when(iz >= 3)(lambda: pl.semaphore_wait(low, 1))
+        pl.when((iz >= 2) & (iz < nz - 1))(lambda: tell(low, iz + 1))
 
         def one(row, carry):
             tell(high.at[iz], row)
@@ -160,22 +165,37 @@
 
         lax.fori_loop(1, iz, one, 0)
 
-    def learn(row):
-        pl.semaphore_wait(high.at[row], 1)
-        pl.when(iz == 1)(lambda: tell(high.at[row], 0))
-        pl.when(iz == 0)(lambda: tell(zero_in, row))
+    def introduce(row):
+        tell(high.at[row], 0)
+        pl.when(jnp.logical_not(middle(row)))(lambda: tell(zero_in, row))
+
+    def introduce_early():
+        def one(row, carry):
+            pl.semaphore_wait(high.at[row], 1)
+            introduce(row)
+            return carry
+
+        lax.fori_loop(2, early + 1, one, 0)
+
+    def introduce_late():
+        pl.semaphore_wait(zero_in, 1)
+        tell(high.at[nz - 1], 0)
+        for row in range(early + 1, nz - 1):
+            introduce(row)
+
+    def meet_all():
+        def one(row, carry):
+            pl.semaphore_wait(high.at[row], 1)
+            return carry
+
+        lax.fori_loop(2, nz, one, 0)
 
     def meet(row):
-        known = (iz <= 1) & (row <= jnp.maximum(early, 1))
-        pl.when((row > iz) & jnp.logical_not(known))(lambda: learn(row))
-        pl.when((row == 0) & (iz >= 2))(lambda: pl.semaphore_wait(zero_in, 1))
-
-    def learn_early():
-        def one(row, carry):
-            learn(row)
-            return carry
-
-        lax.fori_loop(2, early + 1, one, 0)
+        known = jnp.where(iz == 0, nz, jnp.where(iz == 1, early, 0))
+        pl.when((row > iz) & (row > known))(lambda: pl.semaphore_wait(high.at[row], 1))
+        pl.when((row == 0) & (iz >= 2) & (iz < nz - 1) & jnp.logical_not(middle(iz)))(
+            lambda: pl.semaphore_wait(zero_in, 1)
+        )
 
     inside = {
         ("row", -1): iz > 0,
@@ -229,15 +249,28 @@
         for i, (dz, dx, *_) in enumerate(table):
             pl.when(exists(dz, dx))(halo(turn, table, i).wait_send)
 
-    def to_other(turn, src, dst):
+    pieces = PIECES
+    share = rows // pieces
+
+    def to_other(turn, src, dst, piece):
         return pltpu.make_async_remote_copy(
-            src_ref=src.at[pl.ds(8, rows)],
-            dst_ref=dst,
-            send_sem=other_ssem.at[turn],
-            recv_sem=other_rsem.at[turn],
+            src_ref=src.at[pl.ds(8 + piece * share, share)],
+            dst_ref=dst.at[pl.ds(piece * share, share)],
+            send_sem=other_ssem.at[turn, piece],
+            recv_sem=other_rsem.at[turn, piece],
             device_id={"layer": 1 - ic},
             device_id_type=MESH,
         )
+
+    def by_piece(body, carry, before=None, after=None):
+        for piece in range(pieces):
+            if before:
+                before(piece)
+            first, stop = piece * share // 8, (piece + 1) * share // 8
+            carry = lax.fori_loop(first, stop, body, carry, unroll=unroll)
+            if after:
+                after(piece)
+        return carry
 
     tile = (8, cols)
     block = (8, 128)
@@ -281,32 +314,32 @@
         moved = pltpu.roll(value, lax.rem(k + 128 - lane, 128), 1)
         return jnp.where(narrow_lane == k, moved, out)
 
-    def look_up(k, carry):
-        klass = cls[at(k), :]
+    def node(k, lanes):
+        klass = cls[at(k), lanes]
         level = [cc_ref[0, i] for i in range(8)]
         for bit in range(3):
-            high = (klass & (1 << bit)) != 0
-            level = [jnp.where(high, b, a) for a, b in zip(level[::2], level[1::2])]
-        cond = level[0]
-        cond_p[at(k, 8), :] = cond
-        across = via_conductance * via[at(k), :].astype(jnp.float32)
-        coupling[at(k), :] = across
-        rest = across + (pad_conductance * pad[at(k), :].astype(jnp.float32) + leakage)
-        base[at(k), :] = rest
-        load = cur[at(k), :]
-        borders = (
-            (cond[:, :128], 0),
-            (cond[:, :128], 1),
-            (rest[:, :128], 0),
-            (load[:, :128], 0),
-            (cond[:, last:], 127),
-            (cond[:, last:], 126),
-            (rest[:, last:], 127),
-            (load[:, last:], 127),
-        )
+            high_bit = (klass & (1 << bit)) != 0
+            level = [jnp.where(high_bit, b, a) for a, b in zip(level[::2], level[1::2])]
+        across = via_conductance * via[at(k), lanes].astype(jnp.float32)
+        rest = pad_conductance * pad[at(k), lanes].astype(jnp.float32) + leakage
+        return level[0], across, across + rest
+
+    def look_up(k, carry):
+        cond_p[at(k, 8), :], coupling[at(k), :], base[at(k), :] = node(k, slice(None))
+        return carry
+
+    def look_up_ends(k, carry):
+        cond, _, rest = node(k, pl.ds(0, 128))
+        load = cur[at(k), 0:128]
+        borders = [(cond, 0), (cond, 1), (rest, 0), (load, 0)]
+        cond, _, rest = node(k, pl.ds(last, 128))
+        load = cur[at(k), last:cols]
+        borders += [(cond, 127), (cond, 126), (rest, 127), (load, 127)]
         return tuple(place(k, *border, out) for border, out in zip(borders, carry))
 
-    packs = lax.fori_loop(0, chunks, look_up, (zero,) * 8, unroll=unroll)
+    look_up(0, 0)
+    look_up(chunks - 1, 0)
+    packs = lax.fori_loop(0, chunks, look_up_ends, (zero,) * 8, unroll=4)
     for i in range(8):
         raw_col[i // 4, i % 4] = packs[i]
     for side, row in ((0, 0), (1, rows - 1)):
@@ -319,12 +352,14 @@
             corner = cond_p[8 + row : 9 + row, col : col + 1]
             raw_corner[2 * side + end] = jnp.broadcast_to(corner, block)
 
-    neighbours = jnp.minimum(iz, 1) + jnp.minimum(nz - 1 - iz, 1)
-    pl.semaphore_wait(barrier, len(greets[0]) + len(greets[1]) * neighbours)
+    pl.semaphore_wait(barrier, len(greets))
     send_halo(0, raw)
     announce()
-    pl.when(iz <= 1)(learn_early)
+    pl.when(iz == 1)(introduce_early)
+    lax.fori_loop(1, chunks - 1, look_up, 0, unroll=unroll)
     take_halo(0, raw)
+    pl.when(iz == 0)(lambda: tell(zero_in, nz - 1))
+    pl.when(iz == nz - 1)(introduce_late)
     for side, row in ((0, 0), (1, rows + 8)):
         cond_p[row : row + 8, :] = jnp.broadcast_to(got_row[side, 0], tile)
 
@@ -349,8 +384,9 @@
         z_p[at(k, 8), :] = value
         return energy + fold(resid * value)
 
-    energy = lax.fori_loop(0, chunks, precondition, zero, unroll=unroll)
-    to_other(0, z_p, zother).start()
+    energy = by_piece(
+        precondition, zero, after=lambda piece: to_other(0, z_p, zother, piece).start()
+    )
 
     def beyond(here, others, rest, load):
         sides = [edge(here, other) for other in others]
@@ -394,7 +430,6 @@
         inner = raw_col[side, 0]
         z_ends.append(beyond(here, (up, down, outer, inner), rest, load))
     z_left, z_right = z_ends
-    to_other(0, z_p, zother).wait_recv()
 
     def image(k, field, lead, left, right, other):
         values = [field[at(k, 8 * i), :] for i in range(3)]
@@ -412,8 +447,12 @@
         left, right = packed(k, nxt, left, right)
         return left, right, curve + fold(value * out)
 
-    left, right, curve = lax.fori_loop(0, chunks, first_image, (zero, zero, zero), unroll=unroll)
-    to_other(1, y_p, yother).start()
+    left, right, curve = by_piece(
+        first_image,
+        (zero, zero, zero),
+        before=lambda piece: to_other(0, z_p, zother, piece).wait_recv(),
+        after=lambda piece: to_other(1, y_p, yother, piece).start(),
+    )
     y_row[0] = y_p[8:9, :]
     y_row[1] = y_p[rows + 7 : rows + 8, :]
     y_col[0] = left
@@ -422,10 +461,10 @@
     energy = jnp.sum(energy, keepdims=True)
     curve = jnp.sum(curve, keepdims=True)
     guess = energy / curve
+    pl.when(iz == 0)(meet_all)
     take_halo(1, image_halo)
     for side, row in ((0, 0), (1, rows + 8)):
         y_p[row : row + 8, :] = jnp.broadcast_to(goty_row[side], tile)
-    to_other(1, y_p, yother).wait_recv()
 
     y_left, y_right = goty_col[0], goty_col[1]
 
@@ -446,7 +485,11 @@
         )
         return tuple(a + fold(b) for a, b in zip(sums, terms))
 
-    sums = lax.fori_loop(0, chunks, second_image, (zero,) * 6, unroll=unroll)
+    sums = by_piece(
+        second_image,
+        (zero,) * 6,
+        before=lambda piece: to_other(1, y_p, yother, piece).wait_recv(),
+    )
 
     line = (1, 128)
     entries = [(S0, energy), (S1, curve), (GUESS, guess)]
@@ -456,32 +499,76 @@
     ]
     record = by_lane(line, entries)
     srec[...] = record
-    near[reach, me] = record
-
-    shifts = [0] + [dz for far in range(1, reach + 1) for dz in (far, -far)]
-    hops = [(dz, i) for dz in shifts for i in range(len(plane)) if dz or i]
+    near[len(plane) + me] = record
+
+    everyone = range(len(plane))
+
+    def several(ref, first, count, semaphore):
+        part = ref.at[pl.ds(first, count)]
+        return pltpu.make_async_remote_copy(
+            src_ref=part,
+            dst_ref=part,
+            send_sem=semaphore,
+            recv_sem=semaphore,
+            device_id=device(1, 0),
+            device_id_type=MESH,
+        )
 
     def close(dz, i):
+        dx, dc = plane[i]
+        where = device(0, dx, dc)
+        where["row"] = lax.rem(iz + dz + nz, nz)
+        spot = dz + 1
         return pltpu.make_async_remote_copy(
             src_ref=srec,
-            dst_ref=near.at[reach - dz, me],
-            send_sem=near_ssem.at[reach - dz, i],
-            recv_sem=near_rsem.at[reach - dz, i],
-            device_id=device(dz, *plane[i]),
+            dst_ref=near.at[spot * len(plane) + me],
+            send_sem=near_ssem.at[spot],
+            recv_sem=near_rsem.at[spot],
+            device_id=where,
             device_id_type=MESH,
         )
 
-    for dz in shifts:
-        if dz:
-            meet(lax.rem(iz + dz + nz, nz))
-        for hop in hops:
-            if hop[0] == dz:
-                close(*hop).start()
-    for hop in hops:
-        if not hop[0]:
-            close(*hop).wait_recv()
-
-    records = near[reach].reshape(len(plane), 128)
+    def close_arrived(spot):
+        count = len(plane) - (spot == 1)
+        several(near, spot * len(plane), count, near_rsem.at[spot]).wait_recv()
+
+    def greet_plane(dz):
+        meet(lax.rem(iz + dz + nz, nz))
+        for i in everyone:
+            close(dz, i).start()
+
+    def greet_up(dz):
+        pl.when(iz + dz >= nz)(lambda: greet_plane(dz))
+
+    def close_left(spot):
+        count = len(plane) - (spot == 1)
+        several(near, 0, count, near_ssem.at[spot]).wait_send()
+
+    turned = jnp.where(iz >= nz - reach, nz - 1 - iz, 0)
+    ups = [1 + lax.rem(i + turned, reach) for i in range(reach)]
+    for i in everyone[1:]:
+        close(0, i).start()
+    for dz in ups:
+        greet_up(dz)
+    pl.when(iz == 1)(lambda: greet_plane(-1))
+    part = pl.ds(mid_first, mids)
+    hand_on = pltpu.make_async_remote_copy(
+        src_ref=zbuf.at[part],
+        dst_ref=zbuf.at[part],
+        send_sem=pass_sem,
+        recv_sem=mid_rsem,
+        device_id={"row": 0},
+        device_id_type=MESH,
+    )
+
+    def pass_on():
+        hand_on.wait_recv()
+        hand_on.start()
+
+    pl.when(iz == 1)(pass_on)
+    close_arrived(1)
+
+    records = near[pl.ds(len(plane), len(plane))].reshape(len(plane), 128)
     joint = pick(records, S0) / pick(records, S1)
     delta = joint - pick(records, GUESS, axis=1)
     first = by_lane(
@@ -498,30 +585,25 @@
     record = jnp.where(lanes_of(line) == GUESS, joint, record)
     zrec[...] = record
 
-    def along_z(row):
+    def along_z(row, received=z_rsem):
         return pltpu.make_async_remote_copy(
             src_ref=zrec,
             dst_ref=zbuf.at[iz],
-            send_sem=z_ssem.at[row],
-            recv_sem=z_rsem.at[iz],
+            send_sem=z_ssem,
+            recv_sem=received,
             device_id={"row": row},
             device_id_type=MESH,
         )
 
-    def from_z(row):
-        return pltpu.make_async_remote_copy(
-            src_ref=zrec,
-            dst_ref=zbuf.at[row],
-            send_sem=z_ssem.at[row],
-            recv_sem=z_rsem.at[row],
-            device_id={"row": row},
-            device_id_type=MESH,
-        )
-
-    def far_rows(first, stop, act):
+    def direct(source, row):
+        near_by = (row + nz - source <= reach) & (row < source)
+        return near_by | ((row == 0) & ((source == 1) | middle(source)))
+
+    def far_rows(first, stop, act, leaving=True):
         def one(row, carry):
-            away = jnp.abs(row - iz)
-            pl.when((away > reach) & (away < nz - reach))(lambda: act(row))
+            pair = (iz, row) if leaving else (row, iz)
+            far = (row != iz) & jnp.logical_not(direct(*pair))
+            pl.when(far)(lambda: act(row))
             return carry
 
         lax.fori_loop(first, stop, one, 0)
@@ -530,16 +612,44 @@
         meet(row)
         along_z(row).start()
 
-    far_rows(1, iz, lambda row: along_z(row).start())
     far_rows(0, jnp.minimum(iz, 1), met_send)
+    pl.when(middle(iz))(lambda: along_z(1, mid_rsem).start())
+    own = jnp.where(middle(iz), 2, 1)
+    far_rows(own, iz, lambda row: along_z(row).start())
     far_rows(iz + 1, nz, met_send)
-    far_rows(0, nz, lambda row: from_z(row).wait_recv())
-    for hop in hops:
-        if hop[0]:
-            close(*hop).wait_recv()
-
-    records = [near[i].reshape(len(plane), 128) for i in range(2 * reach + 1)]
-    records = jnp.concatenate(records + [zbuf[...].reshape(nz, 128)], axis=0)
+
+    end_halo(0, raw)
+    end_halo(1, image_halo)
+    for piece in range(pieces):
+        to_other(0, z_p, zother, piece).wait_send()
+        to_other(1, y_p, yother, piece).wait_send()
+    close_left(1)
+    pl.when(iz == 1)(lambda: close_left(0))
+    for step in range(1, reach + 1):
+        pl.when(iz + step >= nz)(lambda step=step: close_left(step + 1))
+
+    def wait_far(row, count, receive):
+        copies = several(zbuf, 0, count, z_rsem if receive else z_ssem)
+        pl.when(row)(copies.wait_recv if receive else copies.wait_send)
+
+    wait_far((iz != 1) & (iz < nz - reach) & jnp.logical_not(middle(iz)), nz - 1, False)
+    wait_far(middle(iz), nz - 2, False)
+    wait_far(iz == 1, nz - 2, False)
+    for step in range(reach):
+        wait_far(iz == nz - 1 - step, nz - 1 - reach + step, False)
+    wait_far(iz == 0, nz - 2 - reach - mids, True)
+    for row in range(1, max(reach, 2)):
+        count = nz - 1 - max(reach - row, 0)
+        wait_far(iz == row, count - mids * (row == 1), True)
+    wait_far(iz >= max(reach, 2), nz - 1, True)
+    pl.when(iz == 0)(hand_on.wait_recv)
+    pl.when(iz == 1)(hand_on.wait_send)
+    pl.when(iz == 0)(lambda: close_arrived(0))
+    for step in range(reach, 0, -1):
+        pl.when(iz < step)(lambda step=step: close_arrived(step + 1))
+
+    records = [near[...].reshape(near.shape[0], 128), zbuf[...].reshape(nz, 128)]
+    records = jnp.concatenate(records, axis=0)
     energy, curve = pick(records, S0), pick(records, S1)
     first_step = energy / curve
     delta = first_step - pick(records, GUESS, axis=1)
@@ -553,14 +663,6 @@
     back = first_step * second_step
     for i, value in enumerate((first_step, both, back)):
         scal_ref[i] = jnp.broadcast_to(value, block)
-
-    end_halo(0, raw)
-    end_halo(1, image_halo)
-    to_other(0, z_p, zother).wait_send()
-    to_other(1, y_p, yother).wait_send()
-    for hop in hops:
-        close(*hop).wait_send()
-    far_rows(0, nz, lambda row: along_z(row).wait_send())
 
 
 def finish(cur, z_p, w, y_p, u, scal, drop_hbm, resid_hbm, worst_hbm, drop, resid, worst, sem):
@@ -599,9 +701,10 @@
     hbm = pl.BlockSpec(memory_space=pltpu.HBM)
     vmem = pl.BlockSpec(memory_space=pltpu.VMEM)
     dma = pltpu.SemaphoreType.DMA
-    scratch = [whole, whole, whole, padded, pltpu.VMEM((4, rows, cols), jnp.float32)]
+    scratch = [pltpu.SMEM(class_conductance.shape, jnp.float32)]
+    scratch += [whole, whole, whole, padded, pltpu.VMEM((4, rows, cols), jnp.float32)]
     scratch += [full] * 5
-    near = (2 * REACH + 1, nx * nc)
+    near = (REACH + 2) * nx * nc
     scratch += [
         pltpu.VMEM((2, 4, 1, cols), jnp.float32),
         pltpu.VMEM((2, 4, 8, 128), jnp.float32),
@@ -613,18 +716,20 @@
     ] * 2
     scratch += [
         pltpu.VMEM((1, 128), jnp.float32),
-        pltpu.VMEM((*near, 1, 128), jnp.float32),
+        pltpu.VMEM((near, 1, 128), jnp.float32),
         pltpu.VMEM((1, 128), jnp.float32),
         pltpu.VMEM((nz, 1, 128), jnp.float32),
-        dma((4,)),
+        dma((5,)),
         dma((2, 8)),
         dma((2, 8)),
-        dma((2,)),
-        dma((2,)),
-        dma(near),
-        dma(near),
-        dma((nz,)),
-        dma((nz,)),
+        dma((2, PIECES)),
+        dma((2, PIECES)),
+        dma((REACH + 2,)),
+        dma((REACH + 2,)),
+        dma,
+        dma,
+        dma,
+        dma,
         pltpu.SemaphoreType.REGULAR,
         pltpu.SemaphoreType.REGULAR,
         pltpu.SemaphoreType.REGULAR((nz,)),
@@ -636,7 +741,7 @@
     solved = pl.pallas_call(
         functools.partial(kernel, nz, nx, nc),
         out_shape=[field, tall, field, tall, field, scalars],
-        in_specs=[hbm, hbm, pl.BlockSpec(memory_space=pltpu.SMEM), hbm, hbm],
+        in_specs=[hbm] * 5,
         out_specs=[vmem] * 6,
         scratch_shapes=scratch,
         compiler_params=pltpu.CompilerParams(

time: 104 us -> 71.7 us (0.69)
  the two profiles are of different devices: /device:TPU:33 before, /device:TPU:40 now
where the time goes in v6:
time: 71.7 us; the launch traced here: 71.5 us
  Pallas kernels  70.9 us (99%)
    pallas_call x1, Pallas kernels, local(): pl.pallas_call(functools.partial(kernel, nz, nx, nc), out_shape=[field, t...  69.6 us

profile of v6, /device:TPU:40, one launch (start us, length us, event | category | flops | bytes accessed | tf_op | source)
XLA Modules:
  0.0 71.5 jit_solution(4205747382400761156)
XLA Ops:
  0.6 69.6 %shard_map.76 = (f32[128,1024]{1,0:T(8,128)S(1)}, f32[144,1024]{1,0:T(8,128)S(1)}, f32[128,1024]{1,0:T(8,128)S(1)}, f32[144,1024]{1,0:T(8,128)S(1)}, f32[128,1024]{1,0:T(8,128)S(1)}, /*index=5*/f32[3,8,128]{2,1,0:T(8,128)S(1)}) custom-call(f32[128,1024]{1,0:T(8,128)} %bitcast.6, s32[128,1024]{1,0:T(8,128)} %bitcast.7, f32[1,8]{1,0:T(1,128)} %cc_hbm.1, ...), custom_call_target="tpu_custom_call" | custom-call | tf_op jit(solution)/shard_map/pallas_call | solution.py:741
  70.3 1.3 %shard_map.77 = (f32[128,1024]{1,0:T(8,128)}, f32[128,1024]{1,0:T(8,128)}, f32[128,1024]{1,0:T(8,128)}) custom-call(f32[128,1024]{1,0:T(8,128)S(1)} %get-tuple-element.12.cur, f32[144,1024]{1,0:T(8,128)S(1)} %get-tuple-element.13.z_p, f32[128,1024]{1,0:T(8,128)S(1)} %get-tuple-element.14.w, f32[144,1024]{1,0:T(8,128)S(1)} %get-tuple-element.15.y_p, ...), custom_call_target="tpu_custom_call" | custom-call | tf_op jit(solution)/shard_map/pallas_call | solution.py:751

commit v7 on v6

--- a/solution.py
+++ b/solution.py
@@ -13,7 +13,7 @@
 pad_conductance = 4.0
 leakage = 0.05
 
-REACH = 3
+REACH = 2
 PIECES = 4
 
 S0, S1, Q0, Q1, Q2, E0, E1, E2, GUESS = range(9)
@@ -104,7 +104,7 @@
 ):
     iz, ix, ic = lax.axis_index("row"), lax.axis_index("col"), lax.axis_index("layer")
     rows, cols = cur.shape
-    unroll = 2
+    unroll = 4
     chunks = rows // 8
     reach = REACH
     me = ix * nc + ic

time: 71.7 us -> 70.4 us (0.982)
  Pallas kernels: 70.9 us -> 69.6 us
    pallas_call x1, Pallas kernels: 69.6 us -> 68.4 us  [local(): pl.pallas_call(functools.partial(kernel, nz, nx, nc), out_shape=[field, t...]
where the time goes in v7:
time: 70.4 us; the launch traced here: 70.3 us
  Pallas kernels  69.6 us (99%)
    pallas_call x1, Pallas kernels, local(): pl.pallas_call(functools.partial(kernel, nz, nx, nc), out_shape=[field, t...  68.4 us

profile of v7, /device:TPU:40, one launch (start us, length us, event | category | flops | bytes accessed | tf_op | source)
XLA Modules:
  0.0 70.3 jit_solution(8509380114644934821)
XLA Ops:
  0.6 68.4 %shard_map.76 = (f32[128,1024]{1,0:T(8,128)S(1)}, f32[144,1024]{1,0:T(8,128)S(1)}, f32[128,1024]{1,0:T(8,128)S(1)}, f32[144,1024]{1,0:T(8,128)S(1)}, f32[128,1024]{1,0:T(8,128)S(1)}, /*index=5*/f32[3,8,128]{2,1,0:T(8,128)S(1)}) custom-call(f32[128,1024]{1,0:T(8,128)} %bitcast.6, s32[128,1024]{1,0:T(8,128)} %bitcast.7, f32[1,8]{1,0:T(1,128)} %cc_hbm.1, ...), custom_call_target="tpu_custom_call" | custom-call | tf_op jit(solution)/shard_map/pallas_call | solution.py:741
  69.0 1.3 %shard_map.77 = (f32[128,1024]{1,0:T(8,128)}, f32[128,1024]{1,0:T(8,128)}, f32[128,1024]{1,0:T(8,128)}) custom-call(f32[128,1024]{1,0:T(8,128)S(1)} %get-tuple-element.12.cur, f32[144,1024]{1,0:T(8,128)S(1)} %get-tuple-element.13.z_p, f32[128,1024]{1,0:T(8,128)S(1)} %get-tuple-element.14.w, f32[144,1024]{1,0:T(8,128)S(1)} %get-tuple-element.15.y_p, ...), custom_call_target="tpu_custom_call" | custom-call | tf_op jit(solution)/shard_map/pallas_call | solution.py:751

commit v8 on v7

--- a/solution.py
+++ b/solution.py
@@ -339,7 +339,7 @@
 
     look_up(0, 0)
     look_up(chunks - 1, 0)
-    packs = lax.fori_loop(0, chunks, look_up_ends, (zero,) * 8, unroll=4)
+    packs = lax.fori_loop(0, chunks, look_up_ends, (zero,) * 8, unroll=8)
     for i in range(8):
         raw_col[i // 4, i % 4] = packs[i]
     for side, row in ((0, 0), (1, rows - 1)):

time: 70.4 us -> 70.4 us (level)
  no operation moved by 1% of the time
where the time goes in v8:
time: 70.4 us; the launch traced here: 70.3 us
  Pallas kernels  69.6 us (99%)
    pallas_call x1, Pallas kernels, local(): pl.pallas_call(functools.partial(kernel, nz, nx, nc), out_shape=[field, t...  68.4 us

profile of v8, /device:TPU:40, one launch (start us, length us, event | category | flops | bytes accessed | tf_op | source)
XLA Modules:
  0.0 70.3 jit_solution(4121806322766239576)
XLA Ops:
  0.6 68.4 %shard_map.76 = (f32[128,1024]{1,0:T(8,128)S(1)}, f32[144,1024]{1,0:T(8,128)S(1)}, f32[128,1024]{1,0:T(8,128)S(1)}, f32[144,1024]{1,0:T(8,128)S(1)}, f32[128,1024]{1,0:T(8,128)S(1)}, /*index=5*/f32[3,8,128]{2,1,0:T(8,128)S(1)}) custom-call(f32[128,1024]{1,0:T(8,128)} %bitcast.6, s32[128,1024]{1,0:T(8,128)} %bitcast.7, f32[1,8]{1,0:T(1,128)} %cc_hbm.1, ...), custom_call_target="tpu_custom_call" | custom-call | tf_op jit(solution)/shard_map/pallas_call | solution.py:741
  69.0 1.3 %shard_map.77 = (f32[128,1024]{1,0:T(8,128)}, f32[128,1024]{1,0:T(8,128)}, f32[128,1024]{1,0:T(8,128)}) custom-call(f32[128,1024]{1,0:T(8,128)S(1)} %get-tuple-element.12.cur, f32[144,1024]{1,0:T(8,128)S(1)} %get-tuple-element.13.z_p, f32[128,1024]{1,0:T(8,128)S(1)} %get-tuple-element.14.w, f32[144,1024]{1,0:T(8,128)S(1)} %get-tuple-element.15.y_p, ...), custom_call_target="tpu_custom_call" | custom-call | tf_op jit(solution)/shard_map/pallas_call | solution.py:751
